TPU v7x, 256 devices: a whole 4x4x8 slice. The times are simulated.
256 devices in a mesh: slab: 128 (over z, x, y), head: 2 (over core).
Axes of the slice: x: 4, y: 4, z: 8, core: 2. Of those that a mesh axis runs over, the one named last changes fastest.
Arguments:
- directions: bfloat16 [2, 32768, 5120], P(None, 'slab', 'head'), may hold values from -0.59765625 to 0.59765625
- magnitudes: float32 [4, 40, 32768], P(None, 'head', 'slab'), may hold values from 4 to 24
- outlier_rows: bfloat16 [16384, 4, 5120], P('slab', None, 'head'), may hold values from -6 to 6
- outlier_counts: int32 [128], P('slab'), may hold values from 64 to 128
- destinations: int32 [16384, 1], P('slab'), may hold values from 0 to 127; in each aligned block of 128 rows (0 to 127, 128 to 255, ...) at most 2 rows name the same one
- retention_order: int32 [128, 256], P('slab'), may hold values from 0 to 255, each once within a row
Outputs:
- restored: bfloat16 [4, 32768, 5120], P(None, 'slab', 'head')
Inputs may be any that keep to these rules, and one draw needn't show every extreme that they name: `outlier_counts`: at least 64 rows of each slab are live. `destinations`: among the 128 rows of one slab at most 2 name the same destination slab. `retention_order`: each slab's row is a permutation of its token positions.
All inputs are finite; a program needn't handle non-finite values.
Results may differ from a plain program's by a relative error of at most 0.0013.
Values may be sent and summed in bfloat16 or wider, within the bound.
No kernel may reach another device: no remote copies, remote signals or barrier semaphores. Data moves between devices by JAX's collectives and lax.ppermute only.
A program may use at most 128 MiB of HBM per device.

v0:
```python
import jax
import jax.numpy as jnp
from jax import lax
from jax.experimental import pallas as pl
from jax.experimental.layout import Layout, with_layout_constraint
from jax.experimental.pallas import tpu as pltpu
from jax.sharding import Mesh
from jax.sharding import PartitionSpec as P


SLAB = ("slab_0", "slab_1", "slab_2")
EMPTY = 2.0**127
WIDTH = 512
DEPTH = 2
SPILL = 5


def pack_kernel(turn, dest_ref, count_ref, rows_ref, out_ref, held, blank, seen, slot, in_sem, out_sem):
    slabs = out_ref.shape[0]
    parts = in_sem.shape[0]
    size = held.shape[0] // parts

    def fetch(p):
        part = pl.ds(p * size, size)
        return pltpu.make_async_copy(rows_ref.at[part], held.at[part], in_sem.at[p])

    for p in range(parts):
        fetch(p).start()
    blank[...] = jnp.full(blank.shape, EMPTY, blank.dtype)

    def clear(i, carry):
        seen[i] = 0
        return carry

    lax.fori_loop(0, slabs, clear, 0, unroll=8)
    live = count_ref[0]

    def number(r, carry):
        d = dest_ref[r]
        j = seen[d]
        seen[d] = j + 1
        slot[r] = jnp.where(j == turn, d, -1)
        return carry

    lax.fori_loop(0, live, number, 0)

    def leave(d, carry):
        @pl.when(seen[d] <= turn)
        def _():
            pltpu.make_async_copy(blank.at[0], out_ref.at[d], out_sem).start()

        return carry

    lax.fori_loop(0, slabs, leave, 0, unroll=4)
    for p in range(parts):
        fetch(p).wait()

    def send(r, carry):
        @pl.when(slot[r] >= 0)
        def _():
            pltpu.make_async_copy(held.at[r], out_ref.at[slot[r]], out_sem).start()

        return carry

    lax.fori_loop(0, live, send, 0)
    pltpu.make_async_copy(out_ref, out_ref, out_sem).wait()


def pack(outlier_rows, destinations, outlier_counts, slab_count, turn):
    row_slots, kinds, features = outlier_rows.shape
    smem = pl.BlockSpec(memory_space=pltpu.SMEM)
    anywhere = pl.BlockSpec(memory_space=pl.ANY)
    return pl.pallas_call(
        lambda *refs: pack_kernel(turn, *refs),
        name="pack",
        in_specs=[smem, smem, anywhere],
        out_specs=anywhere,
        out_shape=jax.ShapeDtypeStruct((slab_count, kinds, features), outlier_rows.dtype),
        scratch_shapes=[
            pltpu.VMEM(outlier_rows.shape, outlier_rows.dtype),
            pltpu.VMEM((1, kinds, features), outlier_rows.dtype),
            pltpu.SMEM((slab_count,), jnp.int32),
            pltpu.SMEM((row_slots,), jnp.int32),
            pltpu.SemaphoreType.DMA((4,)),
            pltpu.SemaphoreType.DMA,
        ],
        cost_estimate=pl.CostEstimate(
            flops=2000000, bytes_accessed=2 * row_slots * kinds * features * 2, transcendentals=0
        ),
    )(destinations[:, 0], outlier_counts, outlier_rows)


def spill_kernel(plane, dest_ref, count_ref, rows_ref, out_ref, seen, later, filled, mark, sem):
    planes = filled.shape[0]
    slabs = plane * planes
    places = out_ref.shape[0]
    cap = places // planes
    kinds = out_ref.shape[1]
    features = rows_ref.shape[2]

    def blank(i, carry):
        out_ref[i] = jnp.full(out_ref.shape[1:], EMPTY, out_ref.dtype)
        mark[i] = plane
        return carry

    lax.fori_loop(0, places, blank, 0)

    def clear(i, carry):
        seen[i] = 0
        return carry

    lax.fori_loop(0, slabs, clear, 0, unroll=8)
    seen[slabs] = 0
    for p in range(planes):
        filled[p] = 0
    live = count_ref[0]

    def number(r, found):
        d = jnp.where(r < live, dest_ref[r], slabs)
        j = seen[d]
        seen[d] = j + 1
        later[found] = r
        return found + jnp.where((j > 0) & (d < slabs), 1, 0)

    found = lax.fori_loop(0, dest_ref.shape[0], number, 0, unroll=8)

    def send(i, started):
        r = later[i]
        d = dest_ref[r]
        p = lax.div(d, plane)
        e = filled[p]
        filled[p] = e + 1

        @pl.when(e < cap)
        def _():
            at = p * cap + e
            mark[at] = d - p * plane
            pltpu.make_async_copy(
                rows_ref.at[r], out_ref.at[at, :, pl.ds(0, features)], sem
            ).start()

        return started + jnp.where(e < cap, 1, 0)

    started = lax.fori_loop(0, found, send, 0)
    most = filled[0]
    for p in range(1, planes):
        most = jnp.maximum(most, filled[p])
    over = jnp.where(most > cap, 2 * plane, 0)

    def label(i, carry):
        value = (mark[i] + over).astype(jnp.float32)
        out_ref[i, :, pl.ds(features, 128)] = jnp.full((kinds, 128), value).astype(out_ref.dtype)
        return carry

    lax.fori_loop(0, places, label, 0)

    def finish(r, carry):
        pltpu.make_async_copy(rows_ref.at[0], out_ref.at[0, :, pl.ds(0, features)], sem).wait()
        return carry

    lax.fori_loop(0, started, finish, 0)


def spill(outlier_rows, destinations, outlier_counts, slab_count, planes):
    _, kinds, features = outlier_rows.shape
    smem = pl.BlockSpec(memory_space=pltpu.SMEM)
    plane = slab_count // planes
    return pl.pallas_call(
        lambda *refs: spill_kernel(plane, *refs),
        name="spill",
        in_specs=[smem, smem, pl.BlockSpec(memory_space=pl.ANY)],
        out_specs=pl.BlockSpec(memory_space=pltpu.VMEM),
        out_shape=jax.ShapeDtypeStruct((planes * SPILL, kinds, features + 128), outlier_rows.dtype),
        scratch_shapes=[
            pltpu.SMEM((slab_count + 1,), jnp.int32),
            pltpu.SMEM((outlier_rows.shape[0] + 1,), jnp.int32),
            pltpu.SMEM((planes,), jnp.int32),
            pltpu.SMEM((planes * SPILL,), jnp.int32),
            pltpu.SemaphoreType.DMA,
        ],
        cost_estimate=pl.CostEstimate(
            flops=2000000, bytes_accessed=4 * planes * SPILL * kinds * features, transcendentals=0
        ),
    )(destinations[:, 0], outlier_counts, outlier_rows)


def relay_kernel(here_ref, in_ref, *out_refs):
    places, kinds, width = in_ref.shape
    count = len(out_refs)
    senders = out_refs[0].shape[0]
    cap = places // senders
    total = places * kinds
    lanes = 128
    rows = in_ref[...].reshape(total, width)
    labels = rows[:, width - lanes :]
    corner = jnp.where(lax.broadcasted_iota(jnp.int32, (8, lanes), 1) == 0, 1.0, 0.0).astype(jnp.bfloat16)
    over = (((1,), (1,)), ((), ()))
    label = lax.dot_general(corner, labels, over, preferred_element_type=jnp.float32)[0:1]
    label = label.astype(jnp.int32)
    full = jnp.max(label, axis=1, keepdims=True) >= 2 * count
    owner = label & (2 * count - 1)
    x, y = here_ref[0], here_ref[1]
    ahead = (((owner >> 2) - x) & 3) * 4 + (((owner & 3) - y) & 3)
    ahead = jnp.where(owner < count, ahead, count)
    part = senders * kinds
    source = lax.broadcasted_iota(jnp.int32, (count * part, total), 1)
    target = lax.broadcasted_iota(jnp.int32, (count * part, total), 0)
    same = source % kinds == target % kinds
    same &= source // (cap * kinds) == target // kinds % senders
    picked = jnp.where(same & (ahead == target // part), 1.0, 0.0)
    some = jnp.max(picked, axis=1, keepdims=True) > 0.5
    picker = picked.astype(jnp.bfloat16)
    step = 512
    for c in range(0, width - lanes, step):
        got = jnp.dot(picker, rows[:, c : c + step], preferred_element_type=jnp.float32)
        got = jnp.where(some, got, EMPTY).astype(in_ref.dtype)
        for o in range(count):
            out_refs[o][:, :, c : c + step] = got[o * part : (o + 1) * part].reshape(senders, kinds, step)
    told = jnp.where(full, 1.0, 0.0) * jnp.ones((part, lanes), jnp.float32)
    told = told.astype(in_ref.dtype).reshape(senders, kinds, lanes)
    for o in range(count):
        out_refs[o][:, :, width - lanes :] = told


def relay(gathered, here, planes, count):
    _, kinds, width = gathered.shape
    return pl.pallas_call(
        relay_kernel,
        name="relay",
        in_specs=[pl.BlockSpec(memory_space=pltpu.SMEM), pl.BlockSpec(memory_space=pltpu.VMEM)],
        out_specs=[pl.BlockSpec(memory_space=pltpu.VMEM)] * count,
        out_shape=[jax.ShapeDtypeStruct((planes, kinds, width), gathered.dtype)] * count,
        cost_estimate=pl.CostEstimate(
            flops=10000000, bytes_accessed=4 * count * planes * kinds * width, transcendentals=0
        ),
    )(here, gathered)


def prepare_kernel(dirs_ref, order_ref, out_ref, rank_ref):
    tokens = dirs_ref.shape[1]
    for v in range(2):
        ahead = pltpu.roll(dirs_ref[v].astype(jnp.float32), tokens - 1, 0)
        out_ref[v] = ahead.astype(out_ref.dtype)

    @pl.when(pl.program_id(0) == 0)
    def _():
        token = lax.broadcasted_iota(jnp.int32, (tokens, tokens), 0)
        number = lax.broadcasted_iota(jnp.int32, (tokens, tokens), 1)
        here = jnp.where(order_ref[...] == token, number, 0).astype(jnp.float32)
        rank = jnp.sum(here, axis=1, keepdims=True).astype(jnp.int32)
        rank_ref[...] = jnp.broadcast_to(rank, rank_ref.shape)


def prepare(directions, order):
    _, tokens, features = directions.shape
    width = 256
    spec = pl.BlockSpec((2, tokens, width), lambda i: (0, 0, i))
    return pl.pallas_call(
        prepare_kernel,
        name="prepare",
        compiler_params=pltpu.CompilerParams(vmem_limit_bytes=16 * 2**20),
        grid=(features // width,),
        in_specs=[spec, pl.BlockSpec((1, tokens), lambda i: (0, 0))],
        out_specs=[spec, pl.BlockSpec((tokens, 128), lambda i: (0, 0))],
        out_shape=[
            jax.ShapeDtypeStruct(directions.shape, directions.dtype),
            jax.ShapeDtypeStruct((tokens, 128), jnp.int32),
        ],
        cost_estimate=pl.CostEstimate(
            flops=20 * tokens * features, bytes_accessed=8 * tokens * features, transcendentals=0
        ),
    )(directions, order)


def place_kernel(
    first, second, order, rank, dirs, mags, edge, out,
    a_buf, k_buf, r_buf, d_buf, m_buf, e_buf, o_buf, placer, covered, wide,
    a_sem, k_sem, r_sem, d_sem, m_sem, e_sem, o_sem,
):
    blocks, kinds, tokens, width = o_buf.shape
    slots = a_buf.shape[1]
    half = slots // 2
    lanes = 128
    chunks = slots // lanes
    heads = width // lanes

    def columns(i):
        return pl.ds(pl.multiple_of(i * width, lanes), width)

    class a_copy:
        def __init__(self, i):
            self.parts = [
                pltpu.make_async_copy(
                    half_of.at[:, :, columns(i)], a_buf.at[i, pl.ds(j * half, half)], a_sem.at[i, j]
                )
                for j, half_of in enumerate((first, second))
            ]

        def start(self):
            for part in self.parts:
                part.start()

        def wait(self):
            for part in self.parts:
                part.wait()

    def d_copy(i):
        return pltpu.make_async_copy(dirs.at[:, :, columns(i)], d_buf.at[i], d_sem.at[i])

    def o_copy(i):
        return pltpu.make_async_copy(o_buf.at[i], out.at[:, :, columns(i)], o_sem.at[i])

    r_copy = pltpu.make_async_copy(rank, r_buf, r_sem)
    k_copy = pltpu.make_async_copy(order, k_buf, k_sem)
    m_copy = pltpu.make_async_copy(mags, m_buf, m_sem)
    e_copy = pltpu.make_async_copy(edge, e_buf, e_sem)
    a_copy(0).start()
    k_copy.start()
    r_copy.start()
    m_copy.start()
    e_copy.start()
    d_copy(0).start()
    for i in range(1, DEPTH):
        a_copy(i).start()
        d_copy(i).start()


    def block(i, carry):
        @pl.when(i + DEPTH < blocks)
        def _():
            a_copy(i + DEPTH).start()
            d_copy(i + DEPTH).start()

        a_copy(i).wait()
        for c in range(heads):
            wide[c] = (
                a_buf[i, :, :, c * lanes : (c + 1) * lanes]
                .reshape(slots * kinds, lanes)
                .astype(jnp.float32)
            )

        @pl.when(i == 0)
        def _():
            corner_of = wide[0, pl.ds(0, slots, stride=kinds), :]
            full = jnp.where(corner_of < EMPTY, 1.0, 0.0).astype(jnp.bfloat16)
            corner = jnp.where(lax.broadcasted_iota(jnp.int32, (8, lanes), 1) == 0, 1.0, 0.0)
            corner = corner.astype(jnp.bfloat16)
            over = (((1,), (1,)), ((), ()))
            filled = [
                lax.dot_general(
                    corner, full[c * lanes : (c + 1) * lanes], over, preferred_element_type=jnp.float32
                )
                for c in range(chunks)
            ]
            run = jnp.sum(sum(filled), axis=1, keepdims=True)[0:1]
            k_copy.wait()
            ahead = []
            for c in range(chunks):
                number = jnp.zeros((8, lanes), jnp.float32)
                for e in range(chunks):
                    earlier = k_buf[e, :, :] < k_buf[2 + c, 0:1, :]
                    number += jnp.dot(
                        filled[e].astype(jnp.bfloat16),
                        jnp.where(earlier, 1.0, 0.0).astype(jnp.bfloat16),
                        preferred_element_type=jnp.float32,
                    )
                ahead.append(jnp.where(filled[c] > 0.5, number, -1.0).astype(jnp.int32))
            r_copy.wait()
            m_copy.wait()
            e_copy.wait()
            place_of = r_buf[...]
            covered[...] = jnp.where(place_of < run.astype(jnp.int32), 1, 0)
            for c in range(chunks):
                placer[:, c * lanes : (c + 1) * lanes] = jnp.where(
                    place_of == ahead[c][0:1], 1.0, 0.0
                ).astype(jnp.bfloat16)

        d_copy(i).wait()
        tail = slice(tokens - 16, tokens)
        last = lax.broadcasted_iota(jnp.int32, (16, width), 0) == 15
        for v in range(2):
            end = d_buf[i, v, tail].astype(jnp.float32)
            end = jnp.where(last, e_buf[v : v + 1, columns(i)], end)
            d_buf[i, v, tail] = end.astype(d_buf.dtype)
        given = e_buf[2:3, pl.ds(pl.multiple_of(i * lanes, lanes), lanes)]
        m_buf[i, tail] = jnp.where(last[:, 0:lanes], given, m_buf[i, tail])
        factors = jnp.where(covered[...] > 0, 0.0, m_buf[i])
        own_dirs = [d_buf[i, v].astype(jnp.float32) for v in range(2)]
        for k in range(kinds):
          for c0 in range(0, heads, 2):
            rows = jnp.concatenate(
                [wide[c, pl.ds(k, slots, stride=kinds), :] for c in range(c0, c0 + 2)], axis=1
            ).astype(jnp.bfloat16)
            both = jnp.dot(placer[...], rows, preferred_element_type=jnp.float32)
            for c in range(c0, c0 + 2):
                part = slice(c * lanes, (c + 1) * lanes)
                got = both[:, (c - c0) * lanes : (c - c0 + 1) * lanes]
                own = factors[:, k * heads + c : k * heads + c + 1] * own_dirs[k % 2][:, part]
                o_buf[i, k, :, part] = (got + own).astype(o_buf.dtype)
        o_copy(i).start()
        return carry

    lax.fori_loop(0, blocks, block, 0)
    for i in range(blocks):
        o_copy(i).wait()


def place(first, second, order, rank, dirs, mags, edge):
    slabs, kinds, features = first.shape
    slots = 2 * slabs
    _, tokens, _ = dirs.shape
    width = WIDTH
    blocks = features // width
    anywhere = pl.BlockSpec(memory_space=pl.ANY)
    return pl.pallas_call(
        place_kernel,
        name="place",
        in_specs=[anywhere] * 7,
        out_specs=anywhere,
        out_shape=jax.ShapeDtypeStruct((kinds, tokens, features), first.dtype),
        scratch_shapes=[
            pltpu.VMEM((blocks, slots, kinds, width), first.dtype),
            pltpu.VMEM(order.shape, order.dtype),
            pltpu.VMEM(rank.shape, rank.dtype),
            pltpu.VMEM((blocks, 2, tokens, width), dirs.dtype),
            pltpu.VMEM(mags.shape, mags.dtype),
            pltpu.VMEM(edge.shape, edge.dtype),
            pltpu.VMEM((blocks, kinds, tokens, width), first.dtype),
            pltpu.VMEM((tokens, slots), jnp.bfloat16),
            pltpu.VMEM((tokens, 128), jnp.int32),
            pltpu.VMEM((width // 128, slots * kinds, 128), jnp.float32),
            pltpu.SemaphoreType.DMA((blocks, 2)),
            pltpu.SemaphoreType.DMA,
            pltpu.SemaphoreType.DMA,
            pltpu.SemaphoreType.DMA((blocks,)),
            pltpu.SemaphoreType.DMA,
            pltpu.SemaphoreType.DMA,
            pltpu.SemaphoreType.DMA((blocks,)),
        ],
        cost_estimate=pl.CostEstimate(
            flops=2 * kinds * tokens * slots * features,
            bytes_accessed=2 * (slots * kinds + 2 * tokens + kinds * tokens) * features,
            transcendentals=0,
        ),
    )(first, second, order, rank, dirs, mags, edge)


def passed_back(block, axis):
    devices = lax.axis_size(axis)
    return lax.ppermute(block, axis, [((i + 1) % devices, i) for i in range(devices)])


def per_device(directions, magnitudes, outlier_rows, outlier_counts, destinations, retention_order):
    slab_count = lax.axis_size(SLAB)
    features = directions.shape[2]
    heads = magnitudes.shape[1]
    planes = lax.axis_size("slab_0")
    plane = ("slab_1", "slab_2")
    wide, deep = lax.axis_size("slab_1"), lax.axis_size("slab_2")
    x, y = lax.axis_index("slab_1"), lax.axis_index("slab_2")

    spilled = spill(outlier_rows, destinations, outlier_counts, slab_count, planes)
    gathered = lax.all_to_all(spilled, "slab_0", split_axis=0, concat_axis=0, tiled=True)
    packed = pack(outlier_rows, destinations, outlier_counts, slab_count, 0)
    packed, gathered = lax.optimization_barrier((packed, gathered))
    first = lax.all_to_all(packed, SLAB, split_axis=0, concat_axis=0, tiled=True)

    sorted_rows = relay(gathered, jnp.stack([x, y]).astype(jnp.int32), planes, wide * deep)
    steps = [(dx, dy) for dx in range(wide) for dy in range(deep)]
    second = []
    for (dx, dy), rows in zip(steps, sorted_rows):
        if (dx, dy) != (0, 0):
            route = [
                (i * deep + j, (i + dx) % wide * deep + (j + dy) % deep)
                for i in range(wide)
                for j in range(deep)
            ]
            rows = lax.ppermute(rows, plane, route)
        second.append(rows)
    second = jnp.concatenate(second, axis=0)
    too_many = jnp.max(second[:, 0, features]) > 0.5

    slabs = jnp.arange(slab_count, dtype=jnp.int32)
    step, z = slabs // planes, slabs % planes
    came = z * (wide * deep) + (x - step // deep) % wide * deep + (y - step % deep) % deep

    def order_of(first_slab, second_slab):
        keys = jnp.stack([2 * first_slab, 2 * second_slab + 1]).astype(jnp.int32)
        return jnp.concatenate(
            [
                jnp.broadcast_to(keys[:, :, None], (2, slab_count, 128)),
                jnp.broadcast_to(keys[:, None, :], (2, slab_count, 128)),
            ]
        )

    blocks = features // WIDTH

    def by_block(block):
        count = block.shape[2]
        block = block.reshape(4, blocks, heads // blocks, count).transpose(1, 3, 0, 2)
        block = block.reshape(blocks, count, 4 * heads // blocks)
        return jnp.pad(block, ((0, 0), (0, 0), (0, 128 - block.shape[2])))

    first_mags = by_block(magnitudes[:, :, :1]).reshape(1, blocks * 128)
    edge = jnp.concatenate(
        [
            directions[:, 0, :].astype(jnp.float32),
            jnp.pad(first_mags, ((0, 1), (0, features - blocks * 128))),
        ]
    )
    edge = passed_back(edge, SLAB)
    factors = by_block(jnp.roll(magnitudes, -1, axis=2))
    factors = with_layout_constraint(factors, Layout(major_to_minor=(0, 1, 2)))
    dirs, rank = prepare(directions, retention_order)
    relayed, direct = order_of(slabs, came), order_of(slabs, slabs)

    def short(_):
        return place(first, second, relayed, rank, dirs, factors, edge)

    def long(_):
        rest = pack(outlier_rows, destinations, outlier_counts, slab_count, 1)
        rest = lax.all_to_all(rest, SLAB, split_axis=0, concat_axis=0, tiled=True)
        return place(first, rest, direct, rank, dirs, factors, edge)

    return lax.cond(too_many, long, short, 0)


def solution(mesh):
    finer = Mesh(
        mesh.devices.reshape(8, 4, 4, mesh.shape["head"]), ("slab_0", "slab_1", "slab_2", "head")
    )
    placed = (
        P(None, SLAB, "head"),
        P(None, "head", SLAB),
        P(SLAB, None, "head"),
        P(SLAB),
        P(SLAB, None),
        P(SLAB, None),
    )
    return jax.shard_map(
        per_device, mesh=finer, in_specs=placed, out_specs=P(None, SLAB, "head"), check_vma=False
    )
```

profile of v0, /device:TPU:178, one launch (start us, length us, event | category | flops | bytes accessed | tf_op | source)
XLA Modules:
  0.0 143.8 jit_solution(785248493528383547)
XLA Ops:
  0.8 3.6 %spill.1 = bf16[40,4,2688]{2,1,0:T(4,128)(2,1)} custom-call(s32[128]{0:T(128)} %bitcast.23, s32[1]{0:T(128)S(6)} %copy.41.refs_1_, bf16[128,4,2560]{2,1,0:T(4,128)(2,1)} %refs_2_.3), custom_call_target="tpu_custom_call" | custom-call | flops 2000000 | bytes 1638400 | tf_op jit(solution)/shard_map/spill/pallas_call | solution.py:168
  4.4 0.0 copy-start.7
  4.4 7.0 %all-to-all-start.1 = ((bf16[40,4,2688]{2,1,0:T(4,128)(2,1)}), bf16[40,4,2688]{2,1,0:T(4,128)(2,1)}, u32[]{:S(2)}, u32[]{:S(2)}) async-start(bf16[40,4,2688]{2,1,0:T(4,128)(2,1)} %spill.1), calls=%async_computation.1 | async-start | bytes 1720320 | tf_op jit(solution)/shard_map/all_to_all | solution.py:463
  11.4 0.1 copy.16
  11.5 0.1 reshape.237
  11.6 0.1 reshape.238
  11.7 0.6 select_maximum_fusion
  12.4 0.4 collective-permute-start.15
  12.8 0.1 slice.16
  12.9 0.1 pad_maximum_fusion
  13.0 1.1 copy.14
  14.1 1.1 pad.12
  15.2 0.0 copy-start.1
  15.3 3.5 %pack.3 = bf16[128,4,2560]{2,1,0:T(4,128)(2,1)} custom-call(s32[128]{0:T(128)S(1)} %bitcast.24, s32[1]{0:T(128)S(6)} %copy.41.refs_1_, bf16[128,4,2560]{2,1,0:T(4,128)(2,1)} %refs_2_.3), custom_call_target="tpu_custom_call" | custom-call | flops 2000000 | bytes 5242880 | tf_op jit(solution)/shard_map/pack/pallas_call | solution.py:73
  18.8 4.4 %prepare.1 = (bf16[2,256,2560]{2,1,0:T(8,128)(2,1)}, s32[256,128]{1,0:T(8,128)}) custom-call(bf16[2,256,2560]{2,1,0:T(8,128)(2,1)S(1)} %copy-done, s32[1,256]{1,0:T(1,128)S(1)} %copy-done.1), custom_call_target="tpu_custom_call" | custom-call | flops 13107200 | bytes 5242880 | tf_op jit(solution)/shard_map/prepare/pallas_call | solution.py:258
  23.2 0.6 pad_add_fusion.4.here_ref
  23.9 0.1 broadcast_in_dim.10
  24.0 0.7 pad_add_fusion.1
  24.7 0.1 broadcast_in_dim.8
  24.8 6.9 %all-to-all-done.1.in_ref = bf16[40,4,2688]{2,1,0:T(4,128)(2,1)} async-done(((bf16[40,4,2688]{2,1,0:T(4,128)(2,1)}), bf16[40,4,2688]{2,1,0:T(4,128)(2,1)}, u32[]{:S(2)}, u32[]{:S(2)}) %all-to-all-start.1) | async-done | bytes 860192 | tf_op jit(solution)/shard_map/all_to_all | solution.py:463
  31.7 13.2 %all-to-all-start.2 = ((bf16[128,4,2560]{2,1,0:T(4,128)(2,1)}), bf16[128,4,2560]{2,1,0:T(4,128)(2,1)}, u32[]{:S(2)}, u32[]{:S(2)}) async-start(bf16[128,4,2560]{2,1,0:T(4,128)(2,1)} %pack.3), calls=%async_computation.2 | async-start | bytes 5242880 | tf_op jit(solution)/shard_map/all_to_all | solution.py:466
  44.9 3.8 %relay.1 = (bf16[8,4,2688]{2,1,0:T(4,128)(2,1)}, bf16[8,4,2688]{2,1,0:T(4,128)(2,1)}, bf16[8,4,2688]{2,1,0:T(4,128)(2,1)}, bf16[8,4,2688]{2,1,0:T(4,128)(2,1)}, ...) custom-call(s32[2]{0:T(128)} %pad_add_fusion.4.here_ref, ...), custom_call_target="tpu_custom_call" | custom-call | flops 10000000 | bytes 5505024 | tf_op jit(solution)/shard_map/relay/pallas_call | solution.py:227
  48.8 1.3 collective-permute-start
  50.0 0.8 collective-permute-start.1
  50.9 1.2 collective-permute-start.2
  52.0 1.5 %collective-permute-start.3 = (bf16[8,4,2688]{2,1,0:T(4,128)(2,1)}, bf16[8,4,2688]{2,1,0:T(4,128)(2,1)S(1)}, u32[]{:S(2)}, u32[]{:S(2)}) collective-permute-start(bf16[8,4,2688]{2,1,0:T(4,128)(2,1)} %get-tuple-element.81), channel_id=1, source_target_pairs={{0,8},{2,10},{4,12},{6,14},{8,16},{10,18},{12,20},{14,22},{16,24},... | collective-permute-start | bytes 516104 | tf_op jit(solution)/shard_map/ppermute | solution.py:478
  53.5 1.1 constant_dynamic-update-slice_fusion.15
  54.7 13.2 %collective-permute-done = bf16[8,4,2688]{2,1,0:T(4,128)(2,1)S(1)} collective-permute-done((bf16[8,4,2688]{2,1,0:T(4,128)(2,1)}, bf16[8,4,2688]{2,1,0:T(4,128)(2,1)S(1)}, u32[]{:S(2)}, u32[]{:S(2)}) %collective-permute-start) | collective-permute-done | bytes 172064 | tf_op jit(solution)/shard_map/ppermute | solution.py:478
  67.9 0.1 constant_dynamic-update-slice_fusion.14
  67.9 2.1 %collective-permute-done.1 = bf16[8,4,2688]{2,1,0:T(4,128)(2,1)S(1)} collective-permute-done((bf16[8,4,2688]{2,1,0:T(4,128)(2,1)}, bf16[8,4,2688]{2,1,0:T(4,128)(2,1)S(1)}, u32[]{:S(2)}, u32[]{:S(2)}) %collective-permute-start.1) | collective-permute-done | bytes 172064 | tf_op jit(solution)/shard_map/ppermute | solution.py:478
  70.0 8.5 %collective-permute-start.5 = (bf16[8,4,2688]{2,1,0:T(4,128)(2,1)}, bf16[8,4,2688]{2,1,0:T(4,128)(2,1)S(1)}, u32[]{:S(2)}, u32[]{:S(2)}) collective-permute-start(bf16[8,4,2688]{2,1,0:T(4,128)(2,1)} %get-tuple-element.83), channel_id=1, source_target_pairs={{0,12},{2,14},{4,8},{6,10},{8,20},{10,22},{12,16},{14,18},{16,28},... | collective-permute-start | bytes 516104 | tf_op jit(solution)/shard_map/ppermute | solution.py:478
  78.5 0.1 constant_dynamic-update-slice_fusion.13
  78.6 0.0 collective-permute-done.2
  78.6 0.1 collective-permute-start.6
  78.7 0.1 constant_dynamic-update-slice_fusion.12
  78.8 3.0 %collective-permute-start.7 = (bf16[8,4,2688]{2,1,0:T(4,128)(2,1)}, bf16[8,4,2688]{2,1,0:T(4,128)(2,1)S(1)}, u32[]{:S(2)}, u32[]{:S(2)}) collective-permute-start(bf16[8,4,2688]{2,1,0:T(4,128)(2,1)} %get-tuple-element.85), channel_id=1, source_target_pairs={{0,16},{2,18},{4,20},{6,22},{8,24},{10,26},{12,28},{14,30},{16,0},... | collective-permute-start | bytes 516104 | tf_op jit(solution)/shard_map/ppermute | solution.py:478
  81.8 0.1 constant_dynamic-update-slice_fusion.11
  81.9 4.4 %collective-permute-start.8 = (bf16[8,4,2688]{2,1,0:T(4,128)(2,1)}, bf16[8,4,2688]{2,1,0:T(4,128)(2,1)S(1)}, u32[]{:S(2)}, u32[]{:S(2)}) collective-permute-start(bf16[8,4,2688]{2,1,0:T(4,128)(2,1)} %get-tuple-element.86), channel_id=1, source_target_pairs={{0,18},{2,20},{4,22},{6,16},{8,26},{10,28},{12,30},{14,24},{16,2},... | collective-permute-start | bytes 516104 | tf_op jit(solution)/shard_map/ppermute | solution.py:478
  86.3 0.1 constant_dynamic-update-slice_fusion.10
  86.4 2.4 %collective-permute-done.5 = bf16[8,4,2688]{2,1,0:T(4,128)(2,1)S(1)} collective-permute-done((bf16[8,4,2688]{2,1,0:T(4,128)(2,1)}, bf16[8,4,2688]{2,1,0:T(4,128)(2,1)S(1)}, u32[]{:S(2)}, u32[]{:S(2)}) %collective-permute-start.5) | collective-permute-done | bytes 172064 | tf_op jit(solution)/shard_map/ppermute | solution.py:478
  88.8 5.7 %collective-permute-start.9 = (bf16[8,4,2688]{2,1,0:T(4,128)(2,1)}, bf16[8,4,2688]{2,1,0:T(4,128)(2,1)S(1)}, u32[]{:S(2)}, u32[]{:S(2)}) collective-permute-start(bf16[8,4,2688]{2,1,0:T(4,128)(2,1)} %get-tuple-element.87), channel_id=1, source_target_pairs={{0,20},{2,22},{4,16},{6,18},{8,28},{10,30},{12,24},{14,26},{16,4},... | collective-permute-start | bytes 516104 | tf_op jit(solution)/shard_map/ppermute | solution.py:478
  94.5 0.1 constant_dynamic-update-slice_fusion.9
  94.6 12.7 %collective-permute-done.6 = bf16[8,4,2688]{2,1,0:T(4,128)(2,1)S(1)} collective-permute-done((bf16[8,4,2688]{2,1,0:T(4,128)(2,1)}, bf16[8,4,2688]{2,1,0:T(4,128)(2,1)S(1)}, u32[]{:S(2)}, u32[]{:S(2)}) %collective-permute-start.6) | collective-permute-done | bytes 172064 | tf_op jit(solution)/shard_map/ppermute | solution.py:478
  107.2 0.1 constant_dynamic-update-slice_fusion.8
  107.4 5.5 %collective-permute-start.11 = (bf16[8,4,2688]{2,1,0:T(4,128)(2,1)S(1)}, bf16[8,4,2688]{2,1,0:T(4,128)(2,1)S(1)}, u32[]{:S(2)}, u32[]{:S(2)}) collective-permute-start(bf16[8,4,2688]{2,1,0:T(4,128)(2,1)S(1)} %copy-done.11), channel_id=1, source_target_pairs={{0,24},{2,26},{4,28},{6,30},{8,0},{10,2},{12,4},{14,6},{16,8},{18,... | collective-permute-start | bytes 516104 | tf_op jit(solution)/shard_map/ppermute | solution.py:478
  112.8 0.1 constant_dynamic-update-slice_fusion.7
  112.9 0.3 collective-permute-start.12
  113.2 0.1 constant_dynamic-update-slice_fusion.6
  113.3 1.3 collective-permute-start.13
  114.6 0.1 constant_dynamic-update-slice_fusion.5
  114.7 2.4 %collective-permute-done.10 = bf16[8,4,2688]{2,1,0:T(4,128)(2,1)S(1)} collective-permute-done((bf16[8,4,2688]{2,1,0:T(4,128)(2,1)}, bf16[8,4,2688]{2,1,0:T(4,128)(2,1)S(1)}, u32[]{:S(2)}, u32[]{:S(2)}) %collective-permute-start.10) | collective-permute-done | bytes 172064 | tf_op jit(solution)/shard_map/ppermute | solution.py:478
  117.1 2.6 %collective-permute-start.14 = (bf16[8,4,2688]{2,1,0:T(4,128)(2,1)S(1)}, bf16[8,4,2688]{2,1,0:T(4,128)(2,1)S(1)}, u32[]{:S(2)}, u32[]{:S(2)}) collective-permute-start(bf16[8,4,2688]{2,1,0:T(4,128)(2,1)S(1)} %copy-done.8), channel_id=1, source_target_pairs={{0,30},{2,24},{4,26},{6,28},{8,6},{10,0},{12,2},{14,4},{16,14},{18... | collective-permute-start | bytes 516104 | tf_op jit(solution)/shard_map/ppermute | solution.py:478
  119.8 0.1 constant_dynamic-update-slice_fusion.4
  119.9 0.1 constant_dynamic-update-slice_fusion.3
  119.9 2.0 %collective-permute-done.12 = bf16[8,4,2688]{2,1,0:T(4,128)(2,1)S(1)} collective-permute-done((bf16[8,4,2688]{2,1,0:T(4,128)(2,1)S(1)}, bf16[8,4,2688]{2,1,0:T(4,128)(2,1)S(1)}, u32[]{:S(2)}, u32[]{:S(2)}) %collective-permute-start.12) | collective-permute-done | bytes 172064 | tf_op jit(solution)/shard_map/ppermute | solution.py:478
  121.9 0.1 constant_dynamic-update-slice_fusion.2
  122.0 2.9 %collective-permute-done.13 = bf16[8,4,2688]{2,1,0:T(4,128)(2,1)S(1)} collective-permute-done((bf16[8,4,2688]{2,1,0:T(4,128)(2,1)S(1)}, bf16[8,4,2688]{2,1,0:T(4,128)(2,1)S(1)}, u32[]{:S(2)}, u32[]{:S(2)}) %collective-permute-start.13) | collective-permute-done | bytes 172064 | tf_op jit(solution)/shard_map/ppermute | solution.py:478
  124.9 0.1 constant_dynamic-update-slice_fusion.1
  125.0 7.6 %collective-permute-done.14 = bf16[8,4,2688]{2,1,0:T(4,128)(2,1)S(1)} collective-permute-done((bf16[8,4,2688]{2,1,0:T(4,128)(2,1)S(1)}, bf16[8,4,2688]{2,1,0:T(4,128)(2,1)S(1)}, u32[]{:S(2)}, u32[]{:S(2)}) %collective-permute-start.14) | collective-permute-done | bytes 172064 | tf_op jit(solution)/shard_map/ppermute | solution.py:478
  132.6 0.1 constant_dynamic-update-slice_fusion
  132.7 1.5 %copy-done.4 = bf16[128,4,2688]{2,1,0:T(4,128)(2,1)} copy-done((bf16[128,4,2688]{2,1,0:T(4,128)(2,1)}, bf16[128,4,2688]{2,1,0:T(4,128)(2,1)S(1)}, u32[]{:S(2)}) %copy-start.4) | copy-done | bytes 2752536
  134.2 0.8 slice_reduce_fusion
  135.7 7.9 %conditional.1 = (bf16[4,256,2560]{2,1,0:T(8,128)(2,1)}) conditional(s32[]{:T(128)} %convert_element_type.15, (bf16[128,4,2560]{2,1,0:T(4,128)(2,1)}, bf16[128,4,2688]{2,1,0:T(4,128)(2,1)}, s32[4,128,128]{2,1,0:T(8,128)S(1)}, s32[256,128]{1,0:T(8,128)}, bf16[2,256,2560]{2,1,0:T(8,128)(2,1)}, /*index=5*/f32[5,256,128]{2,1,0:T(8,128)S(1)}, ...), branch_computations={%region_1.2_spmd, %region_2.3_spmd} | conditional | flops 1344177280 | bytes 35127360 | solution.py:525
  135.7 7.9 %place.2 = bf16[4,256,2560]{2,1,0:T(8,128)(2,1)} custom-call(bf16[128,4,2560]{2,1,0:T(4,128)(2,1)} %get-tuple-element.40.first, bf16[128,4,2688]{2,1,0:T(4,128)(2,1)} %get-tuple-element.41.second, s32[4,128,128]{2,1,0:T(8,128)S(1)} %get-tuple-element.42.order, s32[256,128]{1,0:T(8,128)} %get-tuple-element.43.rank, ...), custom_call_target="tpu_custom_call" | custom-call | flops 1342177280 | bytes 13107200 | tf_op jit(solution)/shard_map/cond/branch_0_fun/place/pallas_call | solution.py:415
  (40 shorter events, 0.2 us)
Async XLA Ops:
  0.0 11.4 %copy-start = (bf16[2,256,2560]{2,1,0:T(8,128)(2,1)S(1)}, bf16[2,256,2560]{2,1,0:T(8,128)(2,1)}, u32[]{:S(2)}) copy-start(bf16[2,256,2560]{2,1,0:T(8,128)(2,1)} %dirs_ref.1) | copy-start | bytes 7864324
  0.0 11.4 %copy-start.6 = (f32[4,20,256]{2,0,1:T(4,128)S(1)}, f32[4,20,256]{2,0,1:T(4,128)}, u32[]{:S(2)}) copy-start(f32[4,20,256]{2,0,1:T(4,128)} %param.9) | copy-start | bytes 245764
  4.4 10.8 %copy-start.7 = (s32[128,1]{0,1:T(1,128)S(1)}, s32[128,1]{0,1:T(1,128)}, u32[]{:S(2)}) copy-start(s32[128,1]{0,1:T(1,128)} %param.12) | copy-start | bytes 1540
  4.4 27.3 %all-to-all-start.1 = ((bf16[40,4,2688]{2,1,0:T(4,128)(2,1)}), bf16[40,4,2688]{2,1,0:T(4,128)(2,1)}, u32[]{:S(2)}, u32[]{:S(2)}) async-start(bf16[40,4,2688]{2,1,0:T(4,128)(2,1)} %spill.1), calls=%async_computation.1 | async-start | bytes 1720320 | tf_op jit(solution)/shard_map/all_to_all | solution.py:463
  12.4 123.3 %collective-permute-start.15 = (f32[4,2560]{1,0:T(4,128)}, f32[4,2560]{1,0:T(4,128)}, u32[]{:S(2)}, u32[]{:S(2)}) collective-permute-start(f32[4,2560]{1,0:T(4,128)} %select_maximum_fusion), channel_id=1, source_target_pairs={{2,0},{4,2},{6,4},{8,6},{10,8},{12,10},{14,12},{16,14},{18,16},{20... | collective-permute-start | bytes 122888 | tf_op jit(solution)/shard_map/ppermute | solution.py:450
  15.2 3.5 %copy-start.1 = (s32[1,256]{1,0:T(1,128)S(1)}, s32[1,256]{1,0:T(1,128)}, u32[]{:S(2)}) copy-start(s32[1,256]{1,0:T(1,128)} %order_ref.1) | copy-start | bytes 3076
  31.7 104.0 %all-to-all-start.2 = ((bf16[128,4,2560]{2,1,0:T(4,128)(2,1)}), bf16[128,4,2560]{2,1,0:T(4,128)(2,1)}, u32[]{:S(2)}, u32[]{:S(2)}) async-start(bf16[128,4,2560]{2,1,0:T(4,128)(2,1)} %pack.3), calls=%async_computation.2 | async-start | bytes 5242880 | tf_op jit(solution)/shard_map/all_to_all | solution.py:466
  48.7 58.6 %copy-start.11 = (bf16[8,4,2688]{2,1,0:T(4,128)(2,1)S(1)}, bf16[8,4,2688]{2,1,0:T(4,128)(2,1)}, u32[]{:S(2)}) copy-start(bf16[8,4,2688]{2,1,0:T(4,128)(2,1)} %get-tuple-element.89) | copy-start | bytes 516100
  48.7 64.2 %copy-start.10 = (bf16[8,4,2688]{2,1,0:T(4,128)(2,1)S(1)}, bf16[8,4,2688]{2,1,0:T(4,128)(2,1)}, u32[]{:S(2)}) copy-start(bf16[8,4,2688]{2,1,0:T(4,128)(2,1)} %get-tuple-element.90) | copy-start | bytes 516100
  48.8 64.5 %copy-start.9 = (bf16[8,4,2688]{2,1,0:T(4,128)(2,1)S(1)}, bf16[8,4,2688]{2,1,0:T(4,128)(2,1)}, u32[]{:S(2)}) copy-start(bf16[8,4,2688]{2,1,0:T(4,128)(2,1)} %get-tuple-element.91) | copy-start | bytes 516100
  48.8 68.3 %copy-start.8 = (bf16[8,4,2688]{2,1,0:T(4,128)(2,1)S(1)}, bf16[8,4,2688]{2,1,0:T(4,128)(2,1)}, u32[]{:S(2)}) copy-start(bf16[8,4,2688]{2,1,0:T(4,128)(2,1)} %get-tuple-element.92) | copy-start | bytes 516100
  48.8 19.1 %collective-permute-start = (bf16[8,4,2688]{2,1,0:T(4,128)(2,1)}, bf16[8,4,2688]{2,1,0:T(4,128)(2,1)S(1)}, u32[]{:S(2)}, u32[]{:S(2)}) collective-permute-start(bf16[8,4,2688]{2,1,0:T(4,128)(2,1)} %get-tuple-element.78), channel_id=1, source_target_pairs={{0,2},{2,4},{4,6},{6,0},{8,10},{10,12},{12,14},{14,8},{16,18},{18,... | collective-permute-start | bytes 516104 | tf_op jit(solution)/shard_map/ppermute | solution.py:478
  50.0 20.0 %collective-permute-start.1 = (bf16[8,4,2688]{2,1,0:T(4,128)(2,1)}, bf16[8,4,2688]{2,1,0:T(4,128)(2,1)S(1)}, u32[]{:S(2)}, u32[]{:S(2)}) collective-permute-start(bf16[8,4,2688]{2,1,0:T(4,128)(2,1)} %get-tuple-element.79), channel_id=1, source_target_pairs={{0,4},{2,6},{4,0},{6,2},{8,12},{10,14},{12,8},{14,10},{16,20},{18,... | collective-permute-start | bytes 516104 | tf_op jit(solution)/shard_map/ppermute | solution.py:478
  50.9 27.7 %collective-permute-start.2 = (bf16[8,4,2688]{2,1,0:T(4,128)(2,1)}, bf16[8,4,2688]{2,1,0:T(4,128)(2,1)S(1)}, u32[]{:S(2)}, u32[]{:S(2)}) collective-permute-start(bf16[8,4,2688]{2,1,0:T(4,128)(2,1)} %get-tuple-element.80), channel_id=1, source_target_pairs={{0,6},{2,0},{4,2},{6,4},{8,14},{10,8},{12,10},{14,12},{16,22},{18,... | collective-permute-start | bytes 516104 | tf_op jit(solution)/shard_map/ppermute | solution.py:478
  52.0 26.7 %collective-permute-start.3 = (bf16[8,4,2688]{2,1,0:T(4,128)(2,1)}, bf16[8,4,2688]{2,1,0:T(4,128)(2,1)S(1)}, u32[]{:S(2)}, u32[]{:S(2)}) collective-permute-start(bf16[8,4,2688]{2,1,0:T(4,128)(2,1)} %get-tuple-element.81), channel_id=1, source_target_pairs={{0,8},{2,10},{4,12},{6,14},{8,16},{10,18},{12,20},{14,22},{16,24},... | collective-permute-start | bytes 516104 | tf_op jit(solution)/shard_map/ppermute | solution.py:478
  53.5 82.2 %copy-start.2 = (bf16[128,4,2560]{2,1,0:T(4,128)(2,1)S(1)}, bf16[128,4,2560]{2,1,0:T(4,128)(2,1)}, u32[]{:S(2)}) copy-start(bf16[128,4,2560]{2,1,0:T(4,128)(2,1)} %refs_2_.3) | copy-start | bytes 7864324
  67.9 14.0 %collective-permute-start.4 = (bf16[8,4,2688]{2,1,0:T(4,128)(2,1)}, bf16[8,4,2688]{2,1,0:T(4,128)(2,1)S(1)}, u32[]{:S(2)}, u32[]{:S(2)}) collective-permute-start(bf16[8,4,2688]{2,1,0:T(4,128)(2,1)} %get-tuple-element.82), channel_id=1, source_target_pairs={{0,10},{2,12},{4,14},{6,8},{8,18},{10,20},{12,22},{14,16},{16,26},... | collective-permute-start | bytes 516104 | tf_op jit(solution)/shard_map/ppermute | solution.py:478
  70.0 18.8 %collective-permute-start.5 = (bf16[8,4,2688]{2,1,0:T(4,128)(2,1)}, bf16[8,4,2688]{2,1,0:T(4,128)(2,1)S(1)}, u32[]{:S(2)}, u32[]{:S(2)}) collective-permute-start(bf16[8,4,2688]{2,1,0:T(4,128)(2,1)} %get-tuple-element.83), channel_id=1, source_target_pairs={{0,12},{2,14},{4,8},{6,10},{8,20},{10,22},{12,16},{14,18},{16,28},... | collective-permute-start | bytes 516104 | tf_op jit(solution)/shard_map/ppermute | solution.py:478
  78.6 28.7 %collective-permute-start.6 = (bf16[8,4,2688]{2,1,0:T(4,128)(2,1)}, bf16[8,4,2688]{2,1,0:T(4,128)(2,1)S(1)}, u32[]{:S(2)}, u32[]{:S(2)}) collective-permute-start(bf16[8,4,2688]{2,1,0:T(4,128)(2,1)} %get-tuple-element.84), channel_id=1, source_target_pairs={{0,14},{2,8},{4,10},{6,12},{8,22},{10,16},{12,18},{14,20},{16,30},... | collective-permute-start | bytes 516104 | tf_op jit(solution)/shard_map/ppermute | solution.py:478
  78.8 28.6 %collective-permute-start.7 = (bf16[8,4,2688]{2,1,0:T(4,128)(2,1)}, bf16[8,4,2688]{2,1,0:T(4,128)(2,1)S(1)}, u32[]{:S(2)}, u32[]{:S(2)}) collective-permute-start(bf16[8,4,2688]{2,1,0:T(4,128)(2,1)} %get-tuple-element.85), channel_id=1, source_target_pairs={{0,16},{2,18},{4,20},{6,22},{8,24},{10,26},{12,28},{14,30},{16,0},... | collective-permute-start | bytes 516104 | tf_op jit(solution)/shard_map/ppermute | solution.py:478
  81.9 31.0 %collective-permute-start.8 = (bf16[8,4,2688]{2,1,0:T(4,128)(2,1)}, bf16[8,4,2688]{2,1,0:T(4,128)(2,1)S(1)}, u32[]{:S(2)}, u32[]{:S(2)}) collective-permute-start(bf16[8,4,2688]{2,1,0:T(4,128)(2,1)} %get-tuple-element.86), channel_id=1, source_target_pairs={{0,18},{2,20},{4,22},{6,16},{8,26},{10,28},{12,30},{14,24},{16,2},... | collective-permute-start | bytes 516104 | tf_op jit(solution)/shard_map/ppermute | solution.py:478
  88.8 24.5 %collective-permute-start.9 = (bf16[8,4,2688]{2,1,0:T(4,128)(2,1)}, bf16[8,4,2688]{2,1,0:T(4,128)(2,1)S(1)}, u32[]{:S(2)}, u32[]{:S(2)}) collective-permute-start(bf16[8,4,2688]{2,1,0:T(4,128)(2,1)} %get-tuple-element.87), channel_id=1, source_target_pairs={{0,20},{2,22},{4,16},{6,18},{8,28},{10,30},{12,24},{14,26},{16,4},... | collective-permute-start | bytes 516104 | tf_op jit(solution)/shard_map/ppermute | solution.py:478
  107.2 9.9 %collective-permute-start.10 = (bf16[8,4,2688]{2,1,0:T(4,128)(2,1)}, bf16[8,4,2688]{2,1,0:T(4,128)(2,1)S(1)}, u32[]{:S(2)}, u32[]{:S(2)}) collective-permute-start(bf16[8,4,2688]{2,1,0:T(4,128)(2,1)} %get-tuple-element.88), channel_id=1, source_target_pairs={{0,22},{2,16},{4,18},{6,20},{8,30},{10,24},{12,26},{14,28},{16,6},... | collective-permute-start | bytes 516104 | tf_op jit(solution)/shard_map/ppermute | solution.py:478
  107.4 12.5 %collective-permute-start.11 = (bf16[8,4,2688]{2,1,0:T(4,128)(2,1)S(1)}, bf16[8,4,2688]{2,1,0:T(4,128)(2,1)S(1)}, u32[]{:S(2)}, u32[]{:S(2)}) collective-permute-start(bf16[8,4,2688]{2,1,0:T(4,128)(2,1)S(1)} %copy-done.11), channel_id=1, source_target_pairs={{0,24},{2,26},{4,28},{6,30},{8,0},{10,2},{12,4},{14,6},{16,8},{18,... | collective-permute-start | bytes 516104 | tf_op jit(solution)/shard_map/ppermute | solution.py:478
  112.9 9.0 %collective-permute-start.12 = (bf16[8,4,2688]{2,1,0:T(4,128)(2,1)S(1)}, bf16[8,4,2688]{2,1,0:T(4,128)(2,1)S(1)}, u32[]{:S(2)}, u32[]{:S(2)}) collective-permute-start(bf16[8,4,2688]{2,1,0:T(4,128)(2,1)S(1)} %copy-done.10), channel_id=1, source_target_pairs={{0,26},{2,28},{4,30},{6,24},{8,2},{10,4},{12,6},{14,0},{16,10},{18... | collective-permute-start | bytes 516104 | tf_op jit(solution)/shard_map/ppermute | solution.py:478
  113.3 11.6 %collective-permute-start.13 = (bf16[8,4,2688]{2,1,0:T(4,128)(2,1)S(1)}, bf16[8,4,2688]{2,1,0:T(4,128)(2,1)S(1)}, u32[]{:S(2)}, u32[]{:S(2)}) collective-permute-start(bf16[8,4,2688]{2,1,0:T(4,128)(2,1)S(1)} %copy-done.9), channel_id=1, source_target_pairs={{0,28},{2,30},{4,24},{6,26},{8,4},{10,6},{12,0},{14,2},{16,12},{18... | collective-permute-start | bytes 516104 | tf_op jit(solution)/shard_map/ppermute | solution.py:478
  117.1 15.5 %collective-permute-start.14 = (bf16[8,4,2688]{2,1,0:T(4,128)(2,1)S(1)}, bf16[8,4,2688]{2,1,0:T(4,128)(2,1)S(1)}, u32[]{:S(2)}, u32[]{:S(2)}) collective-permute-start(bf16[8,4,2688]{2,1,0:T(4,128)(2,1)S(1)} %copy-done.8), channel_id=1, source_target_pairs={{0,30},{2,24},{4,26},{6,28},{8,6},{10,0},{12,2},{14,4},{16,14},{18... | collective-permute-start | bytes 516104 | tf_op jit(solution)/shard_map/ppermute | solution.py:478
  132.6 1.5 %copy-start.4 = (bf16[128,4,2688]{2,1,0:T(4,128)(2,1)}, bf16[128,4,2688]{2,1,0:T(4,128)(2,1)S(1)}, u32[]{:S(2)}) copy-start(bf16[128,4,2688]{2,1,0:T(4,128)(2,1)S(1)} %constant_dynamic-update-slice_fusion) | copy-start | bytes 8257540
where the time goes:
time: 144 us
  starting transfers between devices  56.8 us (39%)
  waiting for transfers between devices  52.1 us (36%)
  Pallas kernels  23.3 us (16%)
  local copies, waits for them, and re-layouts  6.72 us (5%)
  other arithmetic  2.93 us (2%)
  between operations  2 us (1%)
    ppermute x15, waiting for transfers between devices, per_device(): rows = lax.ppermute(rows, plane, route)  45.3 us
    ppermute x15, starting transfers between devices, per_device(): rows = lax.ppermute(rows, plane, route)  36.2 us
    all_to_all x1, starting transfers between devices, per_device(): lax.all_to_all(packed, SLAB, split_axis=0, concat_axis=0, tiled=True)  13.2 us
    pallas_call x1, Pallas kernels, place(): pl.pallas_call(place_kernel, name='place', in_specs=[anywhere] * 7, out_s...  7.91 us
    all_to_all x1, starting transfers between devices, per_device(): lax.all_to_all(spilled, 'slab_0', split_axis=0, concat_axis=0, tiled=True)  6.96 us
    all_to_all x1, waiting for transfers between devices, per_device(): lax.all_to_all(spilled, 'slab_0', split_axis=0, concat_axis=0, tiled=True)  6.85 us
    pallas_call x1, Pallas kernels, prepare(): pl.pallas_call(prepare_kernel, name='prepare', compiler_params=pltpu.Comp...  4.42 us
    pallas_call x1, Pallas kernels, relay(): pl.pallas_call(relay_kernel, name='relay', in_specs=[pl.BlockSpec(memory_...  3.82 us
  transfers between devices with their start and end apart: 18, of which 9 were waited for; matrix products, arithmetic and copies ran while one was open for 6% of the time, Pallas kernels for 8%

commit v1 on v0

--- a/solution.py
+++ b/solution.py
@@ -187,7 +187,7 @@
 def relay_kernel(here_ref, in_ref, *out_refs):
     places, kinds, width = in_ref.shape
     count = len(out_refs)
-    senders = out_refs[0].shape[0]
+    senders = out_refs[0].shape[0] // kinds
     cap = places // senders
     total = places * kinds
     lanes = 128
@@ -215,11 +215,11 @@
         got = jnp.dot(picker, rows[:, c : c + step], preferred_element_type=jnp.float32)
         got = jnp.where(some, got, EMPTY).astype(in_ref.dtype)
         for o in range(count):
-            out_refs[o][:, :, c : c + step] = got[o * part : (o + 1) * part].reshape(senders, kinds, step)
+            out_refs[o][:, c : c + step] = got[o * part : (o + 1) * part]
     told = jnp.where(full, 1.0, 0.0) * jnp.ones((part, lanes), jnp.float32)
-    told = told.astype(in_ref.dtype).reshape(senders, kinds, lanes)
+    told = told.astype(in_ref.dtype)
     for o in range(count):
-        out_refs[o][:, :, width - lanes :] = told
+        out_refs[o][:, width - lanes :] = told
 
 
 def relay(gathered, here, planes, count):
@@ -229,7 +229,7 @@
         name="relay",
         in_specs=[pl.BlockSpec(memory_space=pltpu.SMEM), pl.BlockSpec(memory_space=pltpu.VMEM)],
         out_specs=[pl.BlockSpec(memory_space=pltpu.VMEM)] * count,
-        out_shape=[jax.ShapeDtypeStruct((planes, kinds, width), gathered.dtype)] * count,
+        out_shape=[jax.ShapeDtypeStruct((planes * kinds, width), gathered.dtype)] * count,
         cost_estimate=pl.CostEstimate(
             flops=10000000, bytes_accessed=4 * count * planes * kinds * width, transcendentals=0
         ),
@@ -274,12 +274,12 @@
 
 def place_kernel(
     first, second, order, rank, dirs, mags, edge, out,
-    a_buf, k_buf, r_buf, d_buf, m_buf, e_buf, o_buf, placer, covered, wide,
+    a_buf, b_buf, k_buf, r_buf, d_buf, m_buf, e_buf, o_buf, placer, covered, wide,
     a_sem, k_sem, r_sem, d_sem, m_sem, e_sem, o_sem,
 ):
     blocks, kinds, tokens, width = o_buf.shape
-    slots = a_buf.shape[1]
-    half = slots // 2
+    half = a_buf.shape[1]
+    slots = 2 * half
     lanes = 128
     chunks = slots // lanes
     heads = width // lanes
@@ -289,12 +289,10 @@
 
     class a_copy:
         def __init__(self, i):
-            self.parts = [
-                pltpu.make_async_copy(
-                    half_of.at[:, :, columns(i)], a_buf.at[i, pl.ds(j * half, half)], a_sem.at[i, j]
-                )
-                for j, half_of in enumerate((first, second))
-            ]
+            self.parts = (
+                pltpu.make_async_copy(first.at[:, :, columns(i)], a_buf.at[i], a_sem.at[i, 0]),
+                pltpu.make_async_copy(second.at[:, columns(i)], b_buf.at[i], a_sem.at[i, 1]),
+            )
 
         def start(self):
             for part in self.parts:
@@ -333,11 +331,11 @@
 
         a_copy(i).wait()
         for c in range(heads):
-            wide[c] = (
-                a_buf[i, :, :, c * lanes : (c + 1) * lanes]
-                .reshape(slots * kinds, lanes)
-                .astype(jnp.float32)
+            part = slice(c * lanes, (c + 1) * lanes)
+            wide[c, : half * kinds] = (
+                a_buf[i, :, :, part].reshape(half * kinds, lanes).astype(jnp.float32)
             )
+            wide[c, half * kinds :] = b_buf[i, :, part].astype(jnp.float32)
 
         @pl.when(i == 0)
         def _():
@@ -419,7 +417,8 @@
         out_specs=anywhere,
         out_shape=jax.ShapeDtypeStruct((kinds, tokens, features), first.dtype),
         scratch_shapes=[
-            pltpu.VMEM((blocks, slots, kinds, width), first.dtype),
+            pltpu.VMEM((blocks, slabs, kinds, width), first.dtype),
+            pltpu.VMEM((blocks, slabs * kinds, width), first.dtype),
             pltpu.VMEM(order.shape, order.dtype),
             pltpu.VMEM(rank.shape, rank.dtype),
             pltpu.VMEM((blocks, 2, tokens, width), dirs.dtype),
@@ -478,7 +477,7 @@
             rows = lax.ppermute(rows, plane, route)
         second.append(rows)
     second = jnp.concatenate(second, axis=0)
-    too_many = jnp.max(second[:, 0, features]) > 0.5
+    too_many = jnp.max(second[:, features]) > 0.5
 
     slabs = jnp.arange(slab_count, dtype=jnp.int32)
     step, z = slabs // planes, slabs % planes
@@ -520,6 +519,7 @@
     def long(_):
         rest = pack(outlier_rows, destinations, outlier_counts, slab_count, 1)
         rest = lax.all_to_all(rest, SLAB, split_axis=0, concat_axis=0, tiled=True)
+        rest = rest.reshape(-1, features)
         return place(first, rest, direct, rank, dirs, factors, edge)
 
     return lax.cond(too_many, long, short, 0)

time: 144 us -> 140 us (0.972)
  the two profiles are of different devices: /device:TPU:178 before, /device:TPU:200 now
where the time goes in v1:
time: 140 us
  starting transfers between devices  75.3 us (54%)
  waiting for transfers between devices  31.2 us (22%)
  Pallas kernels  23 us (16%)
  local copies, waits for them, and re-layouts  5.78 us (4%)
  other arithmetic  2.78 us (2%)
  between operations  1.89 us (1%)
    ppermute x15, starting transfers between devices, per_device(): rows = lax.ppermute(rows, plane, route)  55.6 us
    ppermute x15, waiting for transfers between devices, per_device(): rows = lax.ppermute(rows, plane, route)  23.8 us
    all_to_all x1, starting transfers between devices, per_device(): lax.all_to_all(packed, SLAB, split_axis=0, concat_axis=0, tiled=True)  12.8 us
    pallas_call x1, Pallas kernels, place(): pl.pallas_call(place_kernel, name='place', in_specs=[anywhere] * 7, out_s...  7.65 us
    all_to_all x1, waiting for transfers between devices, per_device(): lax.all_to_all(spilled, 'slab_0', split_axis=0, concat_axis=0, tiled=True)  7.4 us
    all_to_all x1, starting transfers between devices, per_device(): lax.all_to_all(spilled, 'slab_0', split_axis=0, concat_axis=0, tiled=True)  6.35 us
    pallas_call x1, Pallas kernels, prepare(): pl.pallas_call(prepare_kernel, name='prepare', compiler_params=pltpu.Comp...  4.44 us
    pallas_call x1, Pallas kernels, relay(): pl.pallas_call(relay_kernel, name='relay', in_specs=[pl.BlockSpec(memory_...  3.69 us
  transfers between devices with their start and end apart: 18, of which 7 were waited for; matrix products, arithmetic and copies ran while one was open for 5% of the time, Pallas kernels for 8%

profile of v1, /device:TPU:200, one launch (start us, length us, event | category | flops | bytes accessed | tf_op | source)
XLA Modules:
  0.0 140.0 jit_solution(276382148950992052)
XLA Ops:
  0.8 3.6 %spill.1 = bf16[40,4,2688]{2,1,0:T(4,128)(2,1)} custom-call(s32[128]{0:T(128)} %bitcast.23, s32[1]{0:T(128)S(6)} %copy.41.refs_1_, bf16[128,4,2560]{2,1,0:T(4,128)(2,1)} %refs_2_.3), custom_call_target="tpu_custom_call" | custom-call | flops 2000000 | bytes 1638400 | tf_op jit(solution)/shard_map/spill/pallas_call | solution.py:168
  4.5 0.0 copy-start.6
  4.5 6.3 %all-to-all-start.1 = ((bf16[40,4,2688]{2,1,0:T(4,128)(2,1)}), bf16[40,4,2688]{2,1,0:T(4,128)(2,1)}, u32[]{:S(2)}, u32[]{:S(2)}) async-start(bf16[40,4,2688]{2,1,0:T(4,128)(2,1)} %spill.1), calls=%async_computation.1 | async-start | bytes 1720320 | tf_op jit(solution)/shard_map/all_to_all | solution.py:462
  10.8 0.0 copy-done
  10.9 0.0 copy-done.5
  10.9 0.1 copy.16
  11.0 0.1 reshape.240
  11.1 0.1 reshape.241
  11.2 0.6 select_maximum_fusion
  11.8 0.5 collective-permute-start.15
  12.3 0.1 slice.16
  12.4 0.1 pad_maximum_fusion
  12.6 1.1 copy.14
  13.7 1.1 pad.12
  14.8 0.0 copy-done.6
  14.8 0.0 copy-start.1
  14.8 3.6 %pack.3 = bf16[128,4,2560]{2,1,0:T(4,128)(2,1)} custom-call(s32[128]{0:T(128)S(1)} %bitcast.24, s32[1]{0:T(128)S(6)} %copy.41.refs_1_, bf16[128,4,2560]{2,1,0:T(4,128)(2,1)} %refs_2_.3), custom_call_target="tpu_custom_call" | custom-call | flops 2000000 | bytes 5242880 | tf_op jit(solution)/shard_map/pack/pallas_call | solution.py:73
  18.4 0.0 copy-done.1
  18.4 4.4 %prepare.1 = (bf16[2,256,2560]{2,1,0:T(8,128)(2,1)}, s32[256,128]{1,0:T(8,128)}) custom-call(bf16[2,256,2560]{2,1,0:T(8,128)(2,1)S(1)} %copy-done, s32[1,256]{1,0:T(1,128)S(1)} %copy-done.1), custom_call_target="tpu_custom_call" | custom-call | flops 13107200 | bytes 5242880 | tf_op jit(solution)/shard_map/prepare/pallas_call | solution.py:258
  22.9 0.6 pad_add_fusion.4.here_ref
  23.5 0.1 broadcast_in_dim.10
  23.6 0.7 pad_add_fusion.1
  24.4 0.1 broadcast_in_dim.8
  24.5 7.4 %all-to-all-done.1.in_ref = bf16[40,4,2688]{2,1,0:T(4,128)(2,1)} async-done(((bf16[40,4,2688]{2,1,0:T(4,128)(2,1)}), bf16[40,4,2688]{2,1,0:T(4,128)(2,1)}, u32[]{:S(2)}, u32[]{:S(2)}) %all-to-all-start.1) | async-done | bytes 860192 | tf_op jit(solution)/shard_map/all_to_all | solution.py:462
  31.9 12.8 %all-to-all-start.2 = ((bf16[128,4,2560]{2,1,0:T(4,128)(2,1)}), bf16[128,4,2560]{2,1,0:T(4,128)(2,1)}, u32[]{:S(2)}, u32[]{:S(2)}) async-start(bf16[128,4,2560]{2,1,0:T(4,128)(2,1)} %pack.3), calls=%async_computation.2 | async-start | bytes 5242880 | tf_op jit(solution)/shard_map/all_to_all | solution.py:465
  44.7 3.7 %relay.1 = (bf16[32,2688]{1,0:T(8,128)(2,1)}, bf16[32,2688]{1,0:T(8,128)(2,1)}, bf16[32,2688]{1,0:T(8,128)(2,1)}, bf16[32,2688]{1,0:T(8,128)(2,1)}, bf16[32,2688...) custom-call(s32[2]{0:T(128)} %pad_add_fusion.4.here_ref, ...), custom_call_target="tpu_custom_call" | custom-call | flops 10000000 | bytes 5505024 | tf_op jit(solution)/shard_map/relay/pallas_call | solution.py:227
  48.4 1.5 %collective-permute-start = (bf16[32,2688]{1,0:T(8,128)(2,1)}, bf16[32,2688]{1,0:T(8,128)(2,1)S(1)}, u32[]{:S(2)}, u32[]{:S(2)}) collective-permute-start(bf16[32,2688]{1,0:T(8,128)(2,1)} %get-tuple-element.78), channel_id=1, source_target_pairs={{0,2},{2,4},{4,6},{6,0},{8,10},{10,12},{12,14},{14,8},{16,18},{18,... | collective-permute-start | bytes 516104 | tf_op jit(solution)/shard_map/ppermute | solution.py:477
  50.0 1.2 collective-permute-start.1
  51.1 2.1 %collective-permute-start.2 = (bf16[32,2688]{1,0:T(8,128)(2,1)}, bf16[32,2688]{1,0:T(8,128)(2,1)S(1)}, u32[]{:S(2)}, u32[]{:S(2)}) collective-permute-start(bf16[32,2688]{1,0:T(8,128)(2,1)} %get-tuple-element.80), channel_id=1, source_target_pairs={{0,6},{2,0},{4,2},{6,4},{8,14},{10,8},{12,10},{14,12},{16,22},{18,... | collective-permute-start | bytes 516104 | tf_op jit(solution)/shard_map/ppermute | solution.py:477
  53.2 1.5 %collective-permute-start.3 = (bf16[32,2688]{1,0:T(8,128)(2,1)}, bf16[32,2688]{1,0:T(8,128)(2,1)S(1)}, u32[]{:S(2)}, u32[]{:S(2)}) collective-permute-start(bf16[32,2688]{1,0:T(8,128)(2,1)} %get-tuple-element.81), channel_id=1, source_target_pairs={{0,8},{2,10},{4,12},{6,14},{8,16},{10,18},{12,20},{14,22},{16,24},... | collective-permute-start | bytes 516104 | tf_op jit(solution)/shard_map/ppermute | solution.py:477
  54.7 1.1 constant_dynamic-update-slice_fusion.15
  55.8 9.9 %collective-permute-done = bf16[32,2688]{1,0:T(8,128)(2,1)S(1)} collective-permute-done((bf16[32,2688]{1,0:T(8,128)(2,1)}, bf16[32,2688]{1,0:T(8,128)(2,1)S(1)}, u32[]{:S(2)}, u32[]{:S(2)}) %collective-permute-start) | collective-permute-done | bytes 172064 | tf_op jit(solution)/shard_map/ppermute | solution.py:477
  65.7 0.0 collective-permute-start.4
  65.7 0.0 collective-permute-done.1
  65.7 0.1 collective-permute-start.5
  65.8 0.3 collective-permute-done.2
  66.2 10.1 %collective-permute-start.6 = (bf16[32,2688]{1,0:T(8,128)(2,1)}, bf16[32,2688]{1,0:T(8,128)(2,1)S(1)}, u32[]{:S(2)}, u32[]{:S(2)}) collective-permute-start(bf16[32,2688]{1,0:T(8,128)(2,1)} %get-tuple-element.84), channel_id=1, source_target_pairs={{0,14},{2,8},{4,10},{6,12},{8,22},{10,16},{12,18},{14,20},{16,30},... | collective-permute-start | bytes 516104 | tf_op jit(solution)/shard_map/ppermute | solution.py:477
  76.3 0.0 collective-permute-done.3
  76.3 0.7 collective-permute-start.7
  77.0 0.0 collective-permute-done.4
  77.1 5.0 %collective-permute-start.8 = (bf16[32,2688]{1,0:T(8,128)(2,1)}, bf16[32,2688]{1,0:T(8,128)(2,1)S(1)}, u32[]{:S(2)}, u32[]{:S(2)}) collective-permute-start(bf16[32,2688]{1,0:T(8,128)(2,1)} %get-tuple-element.86), channel_id=1, source_target_pairs={{0,18},{2,20},{4,22},{6,16},{8,26},{10,28},{12,30},{14,24},{16,2},... | collective-permute-start | bytes 516104 | tf_op jit(solution)/shard_map/ppermute | solution.py:477
  82.1 0.0 collective-permute-done.5
  82.1 9.8 %collective-permute-start.9 = (bf16[32,2688]{1,0:T(8,128)(2,1)}, bf16[32,2688]{1,0:T(8,128)(2,1)S(1)}, u32[]{:S(2)}, u32[]{:S(2)}) collective-permute-start(bf16[32,2688]{1,0:T(8,128)(2,1)} %get-tuple-element.87), channel_id=1, source_target_pairs={{0,20},{2,22},{4,16},{6,18},{8,28},{10,30},{12,24},{14,26},{16,4},... | collective-permute-start | bytes 516104 | tf_op jit(solution)/shard_map/ppermute | solution.py:477
  91.9 0.0 collective-permute-done.6
  91.9 18.4 %collective-permute-start.10 = (bf16[32,2688]{1,0:T(8,128)(2,1)}, bf16[32,2688]{1,0:T(8,128)(2,1)S(1)}, u32[]{:S(2)}, u32[]{:S(2)}) collective-permute-start(bf16[32,2688]{1,0:T(8,128)(2,1)} %get-tuple-element.88), channel_id=1, source_target_pairs={{0,22},{2,16},{4,18},{6,20},{8,30},{10,24},{12,26},{14,28},{16,6},... | collective-permute-start | bytes 516104 | tf_op jit(solution)/shard_map/ppermute | solution.py:477
  110.4 0.0 collective-permute-done.7
  110.4 0.1 collective-permute-start.11
  110.5 0.0 collective-permute-done.8
  110.5 0.0 copy-done.9
  110.5 0.3 collective-permute-start.12
  110.9 0.0 collective-permute-done.9
  110.9 1.9 %collective-permute-start.13 = (bf16[32,2688]{1,0:T(8,128)(2,1)S(1)}, bf16[32,2688]{1,0:T(8,128)(2,1)S(1)}, u32[]{:S(2)}, u32[]{:S(2)}) collective-permute-start(bf16[32,2688]{1,0:T(8,128)(2,1)S(1)} %copy-done.8), channel_id=1, source_target_pairs={{0,28},{2,30},{4,24},{6,26},{8,4},{10,6},{12,0},{14,2},{16,12},{18... | collective-permute-start | bytes 516104 | tf_op jit(solution)/shard_map/ppermute | solution.py:477
  112.8 0.8 collective-permute-done.10
  113.6 2.9 %collective-permute-start.14 = (bf16[32,2688]{1,0:T(8,128)(2,1)S(1)}, bf16[32,2688]{1,0:T(8,128)(2,1)S(1)}, u32[]{:S(2)}, u32[]{:S(2)}) collective-permute-start(bf16[32,2688]{1,0:T(8,128)(2,1)S(1)} %copy-done.7), channel_id=1, source_target_pairs={{0,30},{2,24},{4,26},{6,28},{8,6},{10,0},{12,2},{14,4},{16,14},{18... | collective-permute-start | bytes 516104 | tf_op jit(solution)/shard_map/ppermute | solution.py:477
  116.5 0.0 collective-permute-done.11
  116.5 5.5 %collective-permute-done.12 = bf16[32,2688]{1,0:T(8,128)(2,1)S(1)} collective-permute-done((bf16[32,2688]{1,0:T(8,128)(2,1)S(1)}, bf16[32,2688]{1,0:T(8,128)(2,1)S(1)}, u32[]{:S(2)}, u32[]{:S(2)}) %collective-permute-start.12) | collective-permute-done | bytes 172064 | tf_op jit(solution)/shard_map/ppermute | solution.py:477
  122.0 1.6 %collective-permute-done.13 = bf16[32,2688]{1,0:T(8,128)(2,1)S(1)} collective-permute-done((bf16[32,2688]{1,0:T(8,128)(2,1)S(1)}, bf16[32,2688]{1,0:T(8,128)(2,1)S(1)}, u32[]{:S(2)}, u32[]{:S(2)}) %collective-permute-start.13) | collective-permute-done | bytes 172064 | tf_op jit(solution)/shard_map/ppermute | solution.py:477
  123.7 5.7 %collective-permute-done.14 = bf16[32,2688]{1,0:T(8,128)(2,1)S(1)} collective-permute-done((bf16[32,2688]{1,0:T(8,128)(2,1)S(1)}, bf16[32,2688]{1,0:T(8,128)(2,1)S(1)}, u32[]{:S(2)}, u32[]{:S(2)}) %collective-permute-start.14) | collective-permute-done | bytes 172064 | tf_op jit(solution)/shard_map/ppermute | solution.py:477
  129.4 1.5 %copy-done.3 = bf16[512,2688]{1,0:T(8,128)(2,1)} copy-done((bf16[512,2688]{1,0:T(8,128)(2,1)}, bf16[512,2688]{1,0:T(8,128)(2,1)S(1)}, u32[]{:S(2)}) %copy-start.3) | copy-done | bytes 2752536
  130.9 0.7 slice_reduce_fusion
  132.1 0.0 collective-permute-done.15
  132.1 0.0 all-to-all-done.2
  132.2 7.7 %conditional.1 = (bf16[4,256,2560]{2,1,0:T(8,128)(2,1)}) conditional(s32[]{:T(128)} %convert_element_type.15, (bf16[128,4,2560]{2,1,0:T(4,128)(2,1)}, bf16[512,2688]{1,0:T(8,128)(2,1)}, s32[4,128,128]{2,1,0:T(8,128)S(1)}, s32[256,128]{1,0:T(8,128)}, bf16[2,256,2560]{2,1,0:T(8,128)(2,1)}, /*index=5*/f32[5,256,128]{2,1,0:T(8,128)S(1)}, ...), branch_computations={%region_1.2_spmd, %region_2.3_spmd} | conditional | flops 1344177280 | bytes 29884452 | solution.py:525
  132.2 7.6 %place.2 = bf16[4,256,2560]{2,1,0:T(8,128)(2,1)} custom-call(bf16[128,4,2560]{2,1,0:T(4,128)(2,1)} %get-tuple-element.40.first, bf16[512,2688]{1,0:T(8,128)(2,1)} %get-tuple-element.41.second, s32[4,128,128]{2,1,0:T(8,128)S(1)} %get-tuple-element.42.order, s32[256,128]{1,0:T(8,128)} %get-tuple-element.43.rank, bf16[2,256,2560]{2,1,0:T(8,128)(2,1)} %get-tuple-element.44.dirs, ...), custom_call_target="tpu_custom_call" | custom-call | flops 1342177280 | bytes 13107200 | tf_op jit(solution)/shard_map/cond/branch_0_fun/place/pallas_call | solution.py:413
  (40 shorter events, 0.5 us)
Async XLA Ops:
  0.0 10.8 %copy-start = (bf16[2,256,2560]{2,1,0:T(8,128)(2,1)S(1)}, bf16[2,256,2560]{2,1,0:T(8,128)(2,1)}, u32[]{:S(2)}) copy-start(bf16[2,256,2560]{2,1,0:T(8,128)(2,1)} %dirs_ref.1) | copy-start | bytes 7864324
  0.0 10.9 %copy-start.5 = (f32[4,20,256]{2,0,1:T(4,128)S(1)}, f32[4,20,256]{2,0,1:T(4,128)}, u32[]{:S(2)}) copy-start(f32[4,20,256]{2,0,1:T(4,128)} %param.9) | copy-start | bytes 245764
  4.5 10.4 %copy-start.6 = (s32[128,1]{0,1:T(1,128)S(1)}, s32[128,1]{0,1:T(1,128)}, u32[]{:S(2)}) copy-start(s32[128,1]{0,1:T(1,128)} %param.12) | copy-start | bytes 1540
  4.5 27.4 %all-to-all-start.1 = ((bf16[40,4,2688]{2,1,0:T(4,128)(2,1)}), bf16[40,4,2688]{2,1,0:T(4,128)(2,1)}, u32[]{:S(2)}, u32[]{:S(2)}) async-start(bf16[40,4,2688]{2,1,0:T(4,128)(2,1)} %spill.1), calls=%async_computation.1 | async-start | bytes 1720320 | tf_op jit(solution)/shard_map/all_to_all | solution.py:462
  11.8 120.3 %collective-permute-start.15 = (f32[4,2560]{1,0:T(4,128)}, f32[4,2560]{1,0:T(4,128)}, u32[]{:S(2)}, u32[]{:S(2)}) collective-permute-start(f32[4,2560]{1,0:T(4,128)} %select_maximum_fusion), channel_id=1, source_target_pairs={{2,0},{4,2},{6,4},{8,6},{10,8},{12,10},{14,12},{16,14},{18,16},{20... | collective-permute-start | bytes 122888 | tf_op jit(solution)/shard_map/ppermute | solution.py:449
  14.8 3.6 %copy-start.1 = (s32[1,256]{1,0:T(1,128)S(1)}, s32[1,256]{1,0:T(1,128)}, u32[]{:S(2)}) copy-start(s32[1,256]{1,0:T(1,128)} %order_ref.1) | copy-start | bytes 3076
  31.9 100.3 %all-to-all-start.2 = ((bf16[128,4,2560]{2,1,0:T(4,128)(2,1)}), bf16[128,4,2560]{2,1,0:T(4,128)(2,1)}, u32[]{:S(2)}, u32[]{:S(2)}) async-start(bf16[128,4,2560]{2,1,0:T(4,128)(2,1)} %pack.3), calls=%async_computation.2 | async-start | bytes 5242880 | tf_op jit(solution)/shard_map/all_to_all | solution.py:465
  48.4 62.0 %copy-start.10 = (bf16[32,2688]{1,0:T(8,128)(2,1)S(1)}, bf16[32,2688]{1,0:T(8,128)(2,1)}, u32[]{:S(2)}) copy-start(bf16[32,2688]{1,0:T(8,128)(2,1)} %get-tuple-element.89) | copy-start | bytes 516100
  48.4 62.1 %copy-start.9 = (bf16[32,2688]{1,0:T(8,128)(2,1)S(1)}, bf16[32,2688]{1,0:T(8,128)(2,1)}, u32[]{:S(2)}) copy-start(bf16[32,2688]{1,0:T(8,128)(2,1)} %get-tuple-element.90) | copy-start | bytes 516100
  48.4 62.5 %copy-start.8 = (bf16[32,2688]{1,0:T(8,128)(2,1)S(1)}, bf16[32,2688]{1,0:T(8,128)(2,1)}, u32[]{:S(2)}) copy-start(bf16[32,2688]{1,0:T(8,128)(2,1)} %get-tuple-element.91) | copy-start | bytes 516100
  48.4 65.2 %copy-start.7 = (bf16[32,2688]{1,0:T(8,128)(2,1)S(1)}, bf16[32,2688]{1,0:T(8,128)(2,1)}, u32[]{:S(2)}) copy-start(bf16[32,2688]{1,0:T(8,128)(2,1)} %get-tuple-element.92) | copy-start | bytes 516100
  48.4 17.3 %collective-permute-start = (bf16[32,2688]{1,0:T(8,128)(2,1)}, bf16[32,2688]{1,0:T(8,128)(2,1)S(1)}, u32[]{:S(2)}, u32[]{:S(2)}) collective-permute-start(bf16[32,2688]{1,0:T(8,128)(2,1)} %get-tuple-element.78), channel_id=1, source_target_pairs={{0,2},{2,4},{4,6},{6,0},{8,10},{10,12},{12,14},{14,8},{16,18},{18,... | collective-permute-start | bytes 516104 | tf_op jit(solution)/shard_map/ppermute | solution.py:477
  50.0 15.7 %collective-permute-start.1 = (bf16[32,2688]{1,0:T(8,128)(2,1)}, bf16[32,2688]{1,0:T(8,128)(2,1)S(1)}, u32[]{:S(2)}, u32[]{:S(2)}) collective-permute-start(bf16[32,2688]{1,0:T(8,128)(2,1)} %get-tuple-element.79), channel_id=1, source_target_pairs={{0,4},{2,6},{4,0},{6,2},{8,12},{10,14},{12,8},{14,10},{16,20},{18,... | collective-permute-start | bytes 516104 | tf_op jit(solution)/shard_map/ppermute | solution.py:477
  51.1 15.0 %collective-permute-start.2 = (bf16[32,2688]{1,0:T(8,128)(2,1)}, bf16[32,2688]{1,0:T(8,128)(2,1)S(1)}, u32[]{:S(2)}, u32[]{:S(2)}) collective-permute-start(bf16[32,2688]{1,0:T(8,128)(2,1)} %get-tuple-element.80), channel_id=1, source_target_pairs={{0,6},{2,0},{4,2},{6,4},{8,14},{10,8},{12,10},{14,12},{16,22},{18,... | collective-permute-start | bytes 516104 | tf_op jit(solution)/shard_map/ppermute | solution.py:477
  53.2 23.1 %collective-permute-start.3 = (bf16[32,2688]{1,0:T(8,128)(2,1)}, bf16[32,2688]{1,0:T(8,128)(2,1)S(1)}, u32[]{:S(2)}, u32[]{:S(2)}) collective-permute-start(bf16[32,2688]{1,0:T(8,128)(2,1)} %get-tuple-element.81), channel_id=1, source_target_pairs={{0,8},{2,10},{4,12},{6,14},{8,16},{10,18},{12,20},{14,22},{16,24},... | collective-permute-start | bytes 516104 | tf_op jit(solution)/shard_map/ppermute | solution.py:477
  54.7 77.4 %copy-start.2 = (bf16[128,4,2560]{2,1,0:T(4,128)(2,1)S(1)}, bf16[128,4,2560]{2,1,0:T(4,128)(2,1)}, u32[]{:S(2)}) copy-start(bf16[128,4,2560]{2,1,0:T(4,128)(2,1)} %refs_2_.3) | copy-start | bytes 7864324
  65.7 11.4 %collective-permute-start.4 = (bf16[32,2688]{1,0:T(8,128)(2,1)}, bf16[32,2688]{1,0:T(8,128)(2,1)S(1)}, u32[]{:S(2)}, u32[]{:S(2)}) collective-permute-start(bf16[32,2688]{1,0:T(8,128)(2,1)} %get-tuple-element.82), channel_id=1, source_target_pairs={{0,10},{2,12},{4,14},{6,8},{8,18},{10,20},{12,22},{14,16},{16,26},... | collective-permute-start | bytes 516104 | tf_op jit(solution)/shard_map/ppermute | solution.py:477
  65.7 16.4 %collective-permute-start.5 = (bf16[32,2688]{1,0:T(8,128)(2,1)}, bf16[32,2688]{1,0:T(8,128)(2,1)S(1)}, u32[]{:S(2)}, u32[]{:S(2)}) collective-permute-start(bf16[32,2688]{1,0:T(8,128)(2,1)} %get-tuple-element.83), channel_id=1, source_target_pairs={{0,12},{2,14},{4,8},{6,10},{8,20},{10,22},{12,16},{14,18},{16,28},... | collective-permute-start | bytes 516104 | tf_op jit(solution)/shard_map/ppermute | solution.py:477
  66.2 25.8 %collective-permute-start.6 = (bf16[32,2688]{1,0:T(8,128)(2,1)}, bf16[32,2688]{1,0:T(8,128)(2,1)S(1)}, u32[]{:S(2)}, u32[]{:S(2)}) collective-permute-start(bf16[32,2688]{1,0:T(8,128)(2,1)} %get-tuple-element.84), channel_id=1, source_target_pairs={{0,14},{2,8},{4,10},{6,12},{8,22},{10,16},{12,18},{14,20},{16,30},... | collective-permute-start | bytes 516104 | tf_op jit(solution)/shard_map/ppermute | solution.py:477
  76.3 34.1 %collective-permute-start.7 = (bf16[32,2688]{1,0:T(8,128)(2,1)}, bf16[32,2688]{1,0:T(8,128)(2,1)S(1)}, u32[]{:S(2)}, u32[]{:S(2)}) collective-permute-start(bf16[32,2688]{1,0:T(8,128)(2,1)} %get-tuple-element.85), channel_id=1, source_target_pairs={{0,16},{2,18},{4,20},{6,22},{8,24},{10,26},{12,28},{14,30},{16,0},... | collective-permute-start | bytes 516104 | tf_op jit(solution)/shard_map/ppermute | solution.py:477
  77.1 33.4 %collective-permute-start.8 = (bf16[32,2688]{1,0:T(8,128)(2,1)}, bf16[32,2688]{1,0:T(8,128)(2,1)S(1)}, u32[]{:S(2)}, u32[]{:S(2)}) collective-permute-start(bf16[32,2688]{1,0:T(8,128)(2,1)} %get-tuple-element.86), channel_id=1, source_target_pairs={{0,18},{2,20},{4,22},{6,16},{8,26},{10,28},{12,30},{14,24},{16,2},... | collective-permute-start | bytes 516104 | tf_op jit(solution)/shard_map/ppermute | solution.py:477
  82.1 28.8 %collective-permute-start.9 = (bf16[32,2688]{1,0:T(8,128)(2,1)}, bf16[32,2688]{1,0:T(8,128)(2,1)S(1)}, u32[]{:S(2)}, u32[]{:S(2)}) collective-permute-start(bf16[32,2688]{1,0:T(8,128)(2,1)} %get-tuple-element.87), channel_id=1, source_target_pairs={{0,20},{2,22},{4,16},{6,18},{8,28},{10,30},{12,24},{14,26},{16,4},... | collective-permute-start | bytes 516104 | tf_op jit(solution)/shard_map/ppermute | solution.py:477
  91.9 21.6 %collective-permute-start.10 = (bf16[32,2688]{1,0:T(8,128)(2,1)}, bf16[32,2688]{1,0:T(8,128)(2,1)S(1)}, u32[]{:S(2)}, u32[]{:S(2)}) collective-permute-start(bf16[32,2688]{1,0:T(8,128)(2,1)} %get-tuple-element.88), channel_id=1, source_target_pairs={{0,22},{2,16},{4,18},{6,20},{8,30},{10,24},{12,26},{14,28},{16,6},... | collective-permute-start | bytes 516104 | tf_op jit(solution)/shard_map/ppermute | solution.py:477
  110.4 6.1 %collective-permute-start.11 = (bf16[32,2688]{1,0:T(8,128)(2,1)S(1)}, bf16[32,2688]{1,0:T(8,128)(2,1)S(1)}, u32[]{:S(2)}, u32[]{:S(2)}) collective-permute-start(bf16[32,2688]{1,0:T(8,128)(2,1)S(1)} %copy-done.10), channel_id=1, source_target_pairs={{0,24},{2,26},{4,28},{6,30},{8,0},{10,2},{12,4},{14,6},{16,8},{18,... | collective-permute-start | bytes 516104 | tf_op jit(solution)/shard_map/ppermute | solution.py:477
  110.5 11.5 %collective-permute-start.12 = (bf16[32,2688]{1,0:T(8,128)(2,1)S(1)}, bf16[32,2688]{1,0:T(8,128)(2,1)S(1)}, u32[]{:S(2)}, u32[]{:S(2)}) collective-permute-start(bf16[32,2688]{1,0:T(8,128)(2,1)S(1)} %copy-done.9), channel_id=1, source_target_pairs={{0,26},{2,28},{4,30},{6,24},{8,2},{10,4},{12,6},{14,0},{16,10},{18... | collective-permute-start | bytes 516104 | tf_op jit(solution)/shard_map/ppermute | solution.py:477
  110.9 12.8 %collective-permute-start.13 = (bf16[32,2688]{1,0:T(8,128)(2,1)S(1)}, bf16[32,2688]{1,0:T(8,128)(2,1)S(1)}, u32[]{:S(2)}, u32[]{:S(2)}) collective-permute-start(bf16[32,2688]{1,0:T(8,128)(2,1)S(1)} %copy-done.8), channel_id=1, source_target_pairs={{0,28},{2,30},{4,24},{6,26},{8,4},{10,6},{12,0},{14,2},{16,12},{18... | collective-permute-start | bytes 516104 | tf_op jit(solution)/shard_map/ppermute | solution.py:477
  113.6 15.8 %collective-permute-start.14 = (bf16[32,2688]{1,0:T(8,128)(2,1)S(1)}, bf16[32,2688]{1,0:T(8,128)(2,1)S(1)}, u32[]{:S(2)}, u32[]{:S(2)}) collective-permute-start(bf16[32,2688]{1,0:T(8,128)(2,1)S(1)} %copy-done.7), channel_id=1, source_target_pairs={{0,30},{2,24},{4,26},{6,28},{8,6},{10,0},{12,2},{14,4},{16,14},{18... | collective-permute-start | bytes 516104 | tf_op jit(solution)/shard_map/ppermute | solution.py:477
  129.4 1.5 %copy-start.3 = (bf16[512,2688]{1,0:T(8,128)(2,1)}, bf16[512,2688]{1,0:T(8,128)(2,1)S(1)}, u32[]{:S(2)}) copy-start(bf16[512,2688]{1,0:T(8,128)(2,1)S(1)} %constant_dynamic-update-slice_fusion) | copy-start | bytes 8257540

commit v2 on v1

--- a/solution.py
+++ b/solution.py
@@ -1,3 +1,5 @@
+import functools
+
 import jax
 import jax.numpy as jnp
 from jax import lax
@@ -273,10 +275,14 @@
 
 
 def place_kernel(
-    first, second, order, rank, dirs, mags, edge, out,
+    pieces, first, order, rank, dirs, mags, edge, *rest_of
+):
+    second, rest_of = rest_of[:pieces], rest_of[pieces:]
+    (
+    out,
     a_buf, b_buf, k_buf, r_buf, d_buf, m_buf, e_buf, o_buf, placer, covered, wide,
     a_sem, k_sem, r_sem, d_sem, m_sem, e_sem, o_sem,
-):
+) = rest_of
     blocks, kinds, tokens, width = o_buf.shape
     half = a_buf.shape[1]
     slots = 2 * half
@@ -289,18 +295,24 @@
 
     class a_copy:
         def __init__(self, i):
-            self.parts = (
-                pltpu.make_async_copy(first.at[:, :, columns(i)], a_buf.at[i], a_sem.at[i, 0]),
-                pltpu.make_async_copy(second.at[:, columns(i)], b_buf.at[i], a_sem.at[i, 1]),
-            )
+            size = b_buf.shape[1] // pieces
+            self.parts = [
+                pltpu.make_async_copy(first.at[:, :, columns(i)], a_buf.at[i], a_sem.at[i, 0])
+            ] + [
+                pltpu.make_async_copy(
+                    piece.at[:, columns(i)], b_buf.at[i, pl.ds(o * size, size)], a_sem.at[i, 1]
+                )
+                for o, piece in enumerate(second)
+            ]
+            self.whole = pltpu.make_async_copy(b_buf.at[i], b_buf.at[i], a_sem.at[i, 1])
 
         def start(self):
             for part in self.parts:
                 part.start()
 
         def wait(self):
-            for part in self.parts:
-                part.wait()
+            self.parts[0].wait()
+            self.whole.wait()
 
     def d_copy(i):
         return pltpu.make_async_copy(dirs.at[:, :, columns(i)], d_buf.at[i], d_sem.at[i])
@@ -411,9 +423,9 @@
     blocks = features // width
     anywhere = pl.BlockSpec(memory_space=pl.ANY)
     return pl.pallas_call(
-        place_kernel,
+        functools.partial(place_kernel, len(second)),
         name="place",
-        in_specs=[anywhere] * 7,
+        in_specs=[anywhere] * (6 + len(second)),
         out_specs=anywhere,
         out_shape=jax.ShapeDtypeStruct((kinds, tokens, features), first.dtype),
         scratch_shapes=[
@@ -441,7 +453,7 @@
             bytes_accessed=2 * (slots * kinds + 2 * tokens + kinds * tokens) * features,
             transcendentals=0,
         ),
-    )(first, second, order, rank, dirs, mags, edge)
+    )(first, order, rank, dirs, mags, edge, *second)
 
 
 def passed_back(block, axis):
@@ -476,8 +488,8 @@
             ]
             rows = lax.ppermute(rows, plane, route)
         second.append(rows)
-    second = jnp.concatenate(second, axis=0)
-    too_many = jnp.max(second[:, features]) > 0.5
+    told = functools.reduce(jnp.maximum, [rows[:, features:] for rows in second])
+    too_many = jnp.max(told) > 0.5
 
     slabs = jnp.arange(slab_count, dtype=jnp.int32)
     step, z = slabs // planes, slabs % planes
@@ -519,7 +531,7 @@
     def long(_):
         rest = pack(outlier_rows, destinations, outlier_counts, slab_count, 1)
         rest = lax.all_to_all(rest, SLAB, split_axis=0, concat_axis=0, tiled=True)
-        rest = rest.reshape(-1, features)
+        rest = jnp.split(rest.reshape(-1, features), len(second))
         return place(first, rest, direct, rank, dirs, factors, edge)
 
     return lax.cond(too_many, long, short, 0)

time: 140 us -> 144 us (1.029)
  the two profiles are of different devices: /device:TPU:200 before, /device:TPU:64 now
where the time goes in v2:
time: 144 us; the launch traced here: 143 us
  starting transfers between devices  80 us (56%)
  waiting for transfers between devices  29.3 us (20%)
  Pallas kernels  23.8 us (17%)
  local copies, waits for them, and re-layouts  4.6 us (3%)
  other arithmetic  3.74 us (3%)
  between operations  1.96 us (1%)
    ppermute x15, starting transfers between devices, per_device(): rows = lax.ppermute(rows, plane, route)  55.1 us
    all_to_all x1, waiting for transfers between devices, per_device(): lax.all_to_all(spilled, 'slab_0', split_axis=0, concat_axis=0, tiled=True)  18.1 us
    all_to_all x1, starting transfers between devices, per_device(): lax.all_to_all(packed, SLAB, split_axis=0, concat_axis=0, tiled=True)  11.1 us
    ppermute x15, waiting for transfers between devices, per_device(): rows = lax.ppermute(rows, plane, route)  11.1 us
    all_to_all x1, starting transfers between devices, per_device(): lax.all_to_all(spilled, 'slab_0', split_axis=0, concat_axis=0, tiled=True)  8.18 us
    pallas_call x1, Pallas kernels, place(): pl.pallas_call(functools.partial(place_kernel, len(second)), name='place'...  7.83 us
    ppermute x1, starting transfers between devices, passed_back(): lax.ppermute(block, axis, [((i + 1) % devices, i) for i in range(devices)])  5.6 us
    pallas_call x1, Pallas kernels, prepare(): pl.pallas_call(prepare_kernel, name='prepare', compiler_params=pltpu.Comp...  4.42 us
  transfers between devices with their start and end apart: 18, of which 6 were waited for; matrix products, arithmetic and copies ran while one was open for 6% of the time, Pallas kernels for 9%

profile of v2, /device:TPU:64, one launch (start us, length us, event | category | flops | bytes accessed | tf_op | source)
XLA Modules:
  0.0 143.4 jit_solution(940667982833286009)
XLA Ops:
  0.8 3.7 %spill.1 = bf16[40,4,2688]{2,1,0:T(4,128)(2,1)} custom-call(s32[128]{0:T(128)} %bitcast.23, s32[1]{0:T(128)S(6)} %copy.26.refs_1_, bf16[128,4,2560]{2,1,0:T(4,128)(2,1)} %refs_2_.3), custom_call_target="tpu_custom_call" | custom-call | flops 2000000 | bytes 1638400 | tf_op jit(solution)/shard_map/spill/pallas_call | solution.py:170
  4.5 8.2 %all-to-all-start.1 = ((bf16[40,4,2688]{2,1,0:T(4,128)(2,1)}), bf16[40,4,2688]{2,1,0:T(4,128)(2,1)S(1)}, u32[]{:S(2)}, u32[]{:S(2)}) async-start(bf16[40,4,2688]{2,1,0:T(4,128)(2,1)} %spill.1), calls=%async_computation.1 | async-start | bytes 1720320 | tf_op jit(solution)/shard_map/all_to_all | solution.py:474
  12.7 0.0 copy-done.2
  12.7 0.0 copy-done.17
  12.7 4.1 %pack.3 = bf16[128,4,2560]{2,1,0:T(4,128)(2,1)} custom-call(s32[128]{0:T(128)S(1)} %bitcast.24, s32[1]{0:T(128)S(6)} %copy.26.refs_1_, bf16[128,4,2560]{2,1,0:T(4,128)(2,1)S(1)} %copy-done.2), custom_call_target="tpu_custom_call" | custom-call | flops 2000000 | bytes 5242880 | tf_op jit(solution)/shard_map/pack/pallas_call | solution.py:75
  16.8 0.0 copy-start
  16.8 18.1 %all-to-all-done.1.in_ref = bf16[40,4,2688]{2,1,0:T(4,128)(2,1)S(1)} async-done(((bf16[40,4,2688]{2,1,0:T(4,128)(2,1)}), bf16[40,4,2688]{2,1,0:T(4,128)(2,1)S(1)}, u32[]{:S(2)}, u32[]{:S(2)}) %all-to-all-start.1) | async-done | bytes 860192 | tf_op jit(solution)/shard_map/all_to_all | solution.py:474
  34.9 11.1 %all-to-all-start.2 = ((bf16[128,4,2560]{2,1,0:T(4,128)(2,1)}), bf16[128,4,2560]{2,1,0:T(4,128)(2,1)}, u32[]{:S(2)}, u32[]{:S(2)}) async-start(bf16[128,4,2560]{2,1,0:T(4,128)(2,1)} %pack.3), calls=%async_computation.2 | async-start | bytes 5242880 | tf_op jit(solution)/shard_map/all_to_all | solution.py:477
  46.1 0.0 copy-start.1
  46.1 0.0 copy-done.4
  46.1 0.0 copy-done
  46.1 0.8 slice.93
  46.9 0.1 copy.16
  47.0 0.1 reshape.254
  47.1 0.1 reshape.255
  47.2 0.7 pad_add_fusion.4.here_ref
  47.9 0.6 select_maximum_fusion
  48.5 3.8 %relay.1 = (bf16[32,2688]{1,0:T(8,128)(2,1)}, bf16[32,2688]{1,0:T(8,128)(2,1)}, bf16[32,2688]{1,0:T(8,128)(2,1)}, bf16[32,2688]{1,0:T(8,128)(2,1)}, bf16[32,2688...) custom-call(s32[2]{0:T(128)} %pad_add_fusion.4.here_ref, ...), custom_call_target="tpu_custom_call" | custom-call | flops 10000000 | bytes 5505024 | tf_op jit(solution)/shard_map/relay/pallas_call | solution.py:229
  52.3 1.5 %collective-permute-start = (bf16[32,2688]{1,0:T(8,128)(2,1)}, bf16[32,2688]{1,0:T(8,128)(2,1)S(1)}, u32[]{:S(2)}, u32[]{:S(2)}) collective-permute-start(bf16[32,2688]{1,0:T(8,128)(2,1)} %get-tuple-element.123), channel_id=1, source_target_pairs={{0,2},{2,4},{4,6},{6,0},{8,10},{10,12},{12,14},{14,8},{16,18},{18,... | collective-permute-start | bytes 516104 | tf_op jit(solution)/shard_map/ppermute | solution.py:489
  53.8 2.7 %collective-permute-start.1 = (bf16[32,2688]{1,0:T(8,128)(2,1)}, bf16[32,2688]{1,0:T(8,128)(2,1)S(1)}, u32[]{:S(2)}, u32[]{:S(2)}) collective-permute-start(bf16[32,2688]{1,0:T(8,128)(2,1)} %get-tuple-element.124), channel_id=1, source_target_pairs={{0,4},{2,6},{4,0},{6,2},{8,12},{10,14},{12,8},{14,10},{16,20},{18,... | collective-permute-start | bytes 516104 | tf_op jit(solution)/shard_map/ppermute | solution.py:489
  56.4 1.5 %collective-permute-start.2 = (bf16[32,2688]{1,0:T(8,128)(2,1)}, bf16[32,2688]{1,0:T(8,128)(2,1)S(1)}, u32[]{:S(2)}, u32[]{:S(2)}) collective-permute-start(bf16[32,2688]{1,0:T(8,128)(2,1)} %get-tuple-element.125), channel_id=1, source_target_pairs={{0,6},{2,0},{4,2},{6,4},{8,14},{10,8},{12,10},{14,12},{16,22},{18,... | collective-permute-start | bytes 516104 | tf_op jit(solution)/shard_map/ppermute | solution.py:489
  57.9 1.5 %collective-permute-start.3 = (bf16[32,2688]{1,0:T(8,128)(2,1)}, bf16[32,2688]{1,0:T(8,128)(2,1)S(1)}, u32[]{:S(2)}, u32[]{:S(2)}) collective-permute-start(bf16[32,2688]{1,0:T(8,128)(2,1)} %get-tuple-element.126), channel_id=1, source_target_pairs={{0,8},{2,10},{4,12},{6,14},{8,16},{10,18},{12,20},{14,22},{16,24},... | collective-permute-start | bytes 516104 | tf_op jit(solution)/shard_map/ppermute | solution.py:489
  59.4 1.5 %collective-permute-start.4 = (bf16[32,2688]{1,0:T(8,128)(2,1)}, bf16[32,2688]{1,0:T(8,128)(2,1)S(1)}, u32[]{:S(2)}, u32[]{:S(2)}) collective-permute-start(bf16[32,2688]{1,0:T(8,128)(2,1)} %get-tuple-element.127), channel_id=1, source_target_pairs={{0,10},{2,12},{4,14},{6,8},{8,18},{10,20},{12,22},{14,16},{16,26},... | collective-permute-start | bytes 516104 | tf_op jit(solution)/shard_map/ppermute | solution.py:489
  60.9 1.6 %collective-permute-done = bf16[32,2688]{1,0:T(8,128)(2,1)S(1)} collective-permute-done((bf16[32,2688]{1,0:T(8,128)(2,1)}, bf16[32,2688]{1,0:T(8,128)(2,1)S(1)}, u32[]{:S(2)}, u32[]{:S(2)}) %collective-permute-start) | collective-permute-done | bytes 172064 | tf_op jit(solution)/shard_map/ppermute | solution.py:489
  62.5 18.0 %collective-permute-start.5 = (bf16[32,2688]{1,0:T(8,128)(2,1)}, bf16[32,2688]{1,0:T(8,128)(2,1)S(1)}, u32[]{:S(2)}, u32[]{:S(2)}) collective-permute-start(bf16[32,2688]{1,0:T(8,128)(2,1)} %get-tuple-element.128), channel_id=1, source_target_pairs={{0,12},{2,14},{4,8},{6,10},{8,20},{10,22},{12,16},{14,18},{16,28},... | collective-permute-start | bytes 516104 | tf_op jit(solution)/shard_map/ppermute | solution.py:489
  80.6 3.0 %collective-permute-done.1 = bf16[32,2688]{1,0:T(8,128)(2,1)S(1)} collective-permute-done((bf16[32,2688]{1,0:T(8,128)(2,1)}, bf16[32,2688]{1,0:T(8,128)(2,1)S(1)}, u32[]{:S(2)}, u32[]{:S(2)}) %collective-permute-start.1) | collective-permute-done | bytes 172064 | tf_op jit(solution)/shard_map/ppermute | solution.py:489
  83.6 0.0 collective-permute-start.6
  83.6 0.0 collective-permute-done.2
  83.6 0.1 collective-permute-start.7
  83.7 0.0 collective-permute-done.3
  83.7 0.0 copy-start.9
  83.7 5.9 %collective-permute-start.8 = (bf16[32,2688]{1,0:T(8,128)(2,1)}, bf16[32,2688]{1,0:T(8,128)(2,1)S(1)}, u32[]{:S(2)}, u32[]{:S(2)}) collective-permute-start(bf16[32,2688]{1,0:T(8,128)(2,1)} %get-tuple-element.131), channel_id=1, source_target_pairs={{0,18},{2,20},{4,22},{6,16},{8,26},{10,28},{12,30},{14,24},{16,2},... | collective-permute-start | bytes 516104 | tf_op jit(solution)/shard_map/ppermute | solution.py:489
  89.6 0.0 collective-permute-done.4
  89.6 4.4 %collective-permute-start.9 = (bf16[32,2688]{1,0:T(8,128)(2,1)}, bf16[32,2688]{1,0:T(8,128)(2,1)S(1)}, u32[]{:S(2)}, u32[]{:S(2)}) collective-permute-start(bf16[32,2688]{1,0:T(8,128)(2,1)} %get-tuple-element.132), channel_id=1, source_target_pairs={{0,20},{2,22},{4,16},{6,18},{8,28},{10,30},{12,24},{14,26},{16,4},... | collective-permute-start | bytes 516104 | tf_op jit(solution)/shard_map/ppermute | solution.py:489
  94.0 1.0 slice.92
  95.0 0.0 copy-done.6
  95.0 0.1 broadcast_in_dim.10
  95.1 0.7 pad_add_fusion.1
  95.8 0.0 collective-permute-done.5
  95.9 0.9 collective-permute-start.10
  96.7 0.1 collective-permute-done.6
  96.8 2.6 %collective-permute-start.11 = (bf16[32,2688]{1,0:T(8,128)(2,1)}, bf16[32,2688]{1,0:T(8,128)(2,1)}, u32[]{:S(2)}, u32[]{:S(2)}) collective-permute-start(bf16[32,2688]{1,0:T(8,128)(2,1)} %get-tuple-element.134), channel_id=1, source_target_pairs={{0,24},{2,26},{4,28},{6,30},{8,0},{10,2},{12,4},{14,6},{16,8},{18,... | collective-permute-start | bytes 516104 | tf_op jit(solution)/shard_map/ppermute | solution.py:489
  99.4 3.2 %collective-permute-done.7 = bf16[32,2688]{1,0:T(8,128)(2,1)S(1)} collective-permute-done((bf16[32,2688]{1,0:T(8,128)(2,1)}, bf16[32,2688]{1,0:T(8,128)(2,1)S(1)}, u32[]{:S(2)}, u32[]{:S(2)}) %collective-permute-start.7) | collective-permute-done | bytes 172064 | tf_op jit(solution)/shard_map/ppermute | solution.py:489
  102.7 12.2 %collective-permute-start.12 = (bf16[32,2688]{1,0:T(8,128)(2,1)}, bf16[32,2688]{1,0:T(8,128)(2,1)}, u32[]{:S(2)}, u32[]{:S(2)}) collective-permute-start(bf16[32,2688]{1,0:T(8,128)(2,1)} %get-tuple-element.135), channel_id=1, source_target_pairs={{0,26},{2,28},{4,30},{6,24},{8,2},{10,4},{12,6},{14,0},{16,10},{18... | collective-permute-start | bytes 516104 | tf_op jit(solution)/shard_map/ppermute | solution.py:489
  114.9 0.0 collective-permute-done.8
  114.9 0.1 collective-permute-start.13
  115.0 0.0 collective-permute-done.9
  115.0 2.2 %collective-permute-start.14 = (bf16[32,2688]{1,0:T(8,128)(2,1)}, bf16[32,2688]{1,0:T(8,128)(2,1)}, u32[]{:S(2)}, u32[]{:S(2)}) collective-permute-start(bf16[32,2688]{1,0:T(8,128)(2,1)} %get-tuple-element.137), channel_id=1, source_target_pairs={{0,30},{2,24},{4,26},{6,28},{8,6},{10,0},{12,2},{14,4},{16,14},{18... | collective-permute-start | bytes 516104 | tf_op jit(solution)/shard_map/ppermute | solution.py:489
  117.2 0.1 pad_maximum_fusion
  117.4 1.1 copy.14
  118.5 1.1 pad.12
  119.7 4.4 %prepare.1 = (bf16[2,256,2560]{2,1,0:T(8,128)(2,1)}, s32[256,128]{1,0:T(8,128)}) custom-call(bf16[2,256,2560]{2,1,0:T(8,128)(2,1)S(1)} %copy-done, s32[1,256]{1,0:T(1,128)S(1)} %copy-done.1), custom_call_target="tpu_custom_call" | custom-call | flops 13107200 | bytes 5242880 | tf_op jit(solution)/shard_map/prepare/pallas_call | solution.py:260
  124.1 0.1 broadcast_in_dim.8
  124.2 0.0 collective-permute-done.10
  124.2 5.6 %collective-permute-start.15 = (f32[4,2560]{1,0:T(4,128)}, f32[4,2560]{1,0:T(4,128)S(1)}, u32[]{:S(2)}, u32[]{:S(2)}) collective-permute-start(f32[4,2560]{1,0:T(4,128)} %select_maximum_fusion), channel_id=1, source_target_pairs={{2,0},{4,2},{6,4},{8,6},{10,8},{12,10},{14,12},{16,14},{18,16},{20... | collective-permute-start | bytes 122888 | tf_op jit(solution)/shard_map/ppermute | solution.py:461
  129.8 0.0 collective-permute-done.11
  129.9 0.0 collective-permute-done.12
  129.9 0.0 collective-permute-done.13
  129.9 3.2 %collective-permute-done.14 = bf16[32,2688]{1,0:T(8,128)(2,1)} collective-permute-done((bf16[32,2688]{1,0:T(8,128)(2,1)}, bf16[32,2688]{1,0:T(8,128)(2,1)}, u32[]{:S(2)}, u32[]{:S(2)}) %collective-permute-start.14) | collective-permute-done | bytes 172064 | tf_op jit(solution)/shard_map/ppermute | solution.py:489
  133.1 1.6 %fusion.1 = bf16[]{:T(256)} fusion(bf16[32,2688]{1,0:T(8,128)(2,1)} %collective-permute-done.14, bf16[32,2688]{1,0:T(8,128)(2,1)} %collective-permute-done.13, bf16[32,2688]{1,0:T(8,128)(2,1)} %collective-permute-done.12, bf16[32,2688]{1,0:T(8,128)(2,1)} %collective-permute-done.11, bf16[32,2688]{1,0:T(8,128)(2,1)} %collective-permute-done.10, ...), kind=kLoop, calls=%fused_computation.9 | loop fusion | flops 65535 | bytes 131074 | tf_op jit(solution)/shard_map/reduce_max | solution.py:492
  135.3 0.0 collective-permute-done.15
  135.4 0.0 all-to-all-done.2
  135.4 7.8 %conditional.1 = (bf16[4,256,2560]{2,1,0:T(8,128)(2,1)}) conditional(s32[]{:T(128)} %convert_element_type.15, (bf16[128,4,2560]{2,1,0:T(4,128)(2,1)}, s32[4,128,128]{2,1,0:T(8,128)S(1)}, s32[256,128]{1,0:T(8,128)}, bf16[2,256,2560]{2,1,0:T(8,128)(2,1)}, f32[5,256,128]{2,1,0:T(8,128)S(1)}, /*index=5*/f32[4,2560]{1,0:T(4,128)S(1)}, ...), branch_computations={%region_1.2_spmd, %region_2.3_spmd} | conditional | flops 1344177280 | bytes 45776988 | solution.py:537
  135.4 7.8 %place.2 = bf16[4,256,2560]{2,1,0:T(8,128)(2,1)} custom-call(bf16[128,4,2560]{2,1,0:T(4,128)(2,1)} %get-tuple-element.70.first, s32[4,128,128]{2,1,0:T(8,128)S(1)} %get-tuple-element.71.order, s32[256,128]{1,0:T(8,128)} %get-tuple-element.72.rank, bf16[2,256,2560]{2,1,0:T(8,128)(2,1)} %get-tuple-element.73.dirs, f32[5,256,128]{2,1,0:T(8,128)S(1)} %get-tuple-element.74.mags, ...), custom_call_target="tpu_custom_call" | custom-call | flops 1342177280 | bytes 13107200 | tf_op jit(solution)/shard_map/cond/branch_0_fun/place/pallas_call | solution.py:425
  (34 shorter events, 0.2 us)
Async XLA Ops:
  0.0 12.7 %copy-start.2 = (bf16[128,4,2560]{2,1,0:T(4,128)(2,1)S(1)}, bf16[128,4,2560]{2,1,0:T(4,128)(2,1)}, u32[]{:S(2)}) copy-start(bf16[128,4,2560]{2,1,0:T(4,128)(2,1)} %refs_2_.3) | copy-start | bytes 7864324
  0.0 12.7 %copy-start.17 = (s32[128,1]{0,1:T(1,128)S(1)}, s32[128,1]{0,1:T(1,128)}, u32[]{:S(2)}) copy-start(s32[128,1]{0,1:T(1,128)} %param.12) | copy-start | bytes 1540
  4.5 30.4 %all-to-all-start.1 = ((bf16[40,4,2688]{2,1,0:T(4,128)(2,1)}), bf16[40,4,2688]{2,1,0:T(4,128)(2,1)S(1)}, u32[]{:S(2)}, u32[]{:S(2)}) async-start(bf16[40,4,2688]{2,1,0:T(4,128)(2,1)} %spill.1), calls=%async_computation.1 | async-start | bytes 1720320 | tf_op jit(solution)/shard_map/all_to_all | solution.py:474
  16.8 29.3 %copy-start = (bf16[2,256,2560]{2,1,0:T(8,128)(2,1)S(1)}, bf16[2,256,2560]{2,1,0:T(8,128)(2,1)}, u32[]{:S(2)}) copy-start(bf16[2,256,2560]{2,1,0:T(8,128)(2,1)} %dirs_ref.1) | copy-start | bytes 7864324
  34.9 11.2 %copy-start.4 = (bf16[40,4,2688]{2,1,0:T(4,128)(2,1)}, bf16[40,4,2688]{2,1,0:T(4,128)(2,1)S(1)}, u32[]{:S(2)}) copy-start(bf16[40,4,2688]{2,1,0:T(4,128)(2,1)S(1)} %all-to-all-done.1.in_ref) | copy-start | bytes 2580484
  34.9 100.4 %all-to-all-start.2 = ((bf16[128,4,2560]{2,1,0:T(4,128)(2,1)}), bf16[128,4,2560]{2,1,0:T(4,128)(2,1)}, u32[]{:S(2)}, u32[]{:S(2)}) async-start(bf16[128,4,2560]{2,1,0:T(4,128)(2,1)} %pack.3), calls=%async_computation.2 | async-start | bytes 5242880 | tf_op jit(solution)/shard_map/all_to_all | solution.py:477
  46.1 73.6 %copy-start.1 = (s32[1,256]{1,0:T(1,128)S(1)}, s32[1,256]{1,0:T(1,128)}, u32[]{:S(2)}) copy-start(s32[1,256]{1,0:T(1,128)} %order_ref.1) | copy-start | bytes 3076
  52.3 10.2 %collective-permute-start = (bf16[32,2688]{1,0:T(8,128)(2,1)}, bf16[32,2688]{1,0:T(8,128)(2,1)S(1)}, u32[]{:S(2)}, u32[]{:S(2)}) collective-permute-start(bf16[32,2688]{1,0:T(8,128)(2,1)} %get-tuple-element.123), channel_id=1, source_target_pairs={{0,2},{2,4},{4,6},{6,0},{8,10},{10,12},{12,14},{14,8},{16,18},{18,... | collective-permute-start | bytes 516104 | tf_op jit(solution)/shard_map/ppermute | solution.py:489
  53.8 29.8 %collective-permute-start.1 = (bf16[32,2688]{1,0:T(8,128)(2,1)}, bf16[32,2688]{1,0:T(8,128)(2,1)S(1)}, u32[]{:S(2)}, u32[]{:S(2)}) collective-permute-start(bf16[32,2688]{1,0:T(8,128)(2,1)} %get-tuple-element.124), channel_id=1, source_target_pairs={{0,4},{2,6},{4,0},{6,2},{8,12},{10,14},{12,8},{14,10},{16,20},{18,... | collective-permute-start | bytes 516104 | tf_op jit(solution)/shard_map/ppermute | solution.py:489
  56.4 27.1 %collective-permute-start.2 = (bf16[32,2688]{1,0:T(8,128)(2,1)}, bf16[32,2688]{1,0:T(8,128)(2,1)S(1)}, u32[]{:S(2)}, u32[]{:S(2)}) collective-permute-start(bf16[32,2688]{1,0:T(8,128)(2,1)} %get-tuple-element.125), channel_id=1, source_target_pairs={{0,6},{2,0},{4,2},{6,4},{8,14},{10,8},{12,10},{14,12},{16,22},{18,... | collective-permute-start | bytes 516104 | tf_op jit(solution)/shard_map/ppermute | solution.py:489
  57.9 25.8 %collective-permute-start.3 = (bf16[32,2688]{1,0:T(8,128)(2,1)}, bf16[32,2688]{1,0:T(8,128)(2,1)S(1)}, u32[]{:S(2)}, u32[]{:S(2)}) collective-permute-start(bf16[32,2688]{1,0:T(8,128)(2,1)} %get-tuple-element.126), channel_id=1, source_target_pairs={{0,8},{2,10},{4,12},{6,14},{8,16},{10,18},{12,20},{14,22},{16,24},... | collective-permute-start | bytes 516104 | tf_op jit(solution)/shard_map/ppermute | solution.py:489
  59.4 30.2 %collective-permute-start.4 = (bf16[32,2688]{1,0:T(8,128)(2,1)}, bf16[32,2688]{1,0:T(8,128)(2,1)S(1)}, u32[]{:S(2)}, u32[]{:S(2)}) collective-permute-start(bf16[32,2688]{1,0:T(8,128)(2,1)} %get-tuple-element.127), channel_id=1, source_target_pairs={{0,10},{2,12},{4,14},{6,8},{8,18},{10,20},{12,22},{14,16},{16,26},... | collective-permute-start | bytes 516104 | tf_op jit(solution)/shard_map/ppermute | solution.py:489
  62.5 32.5 %copy-start.6 = (bf16[32,2688]{1,0:T(8,128)(2,1)}, bf16[32,2688]{1,0:T(8,128)(2,1)S(1)}, u32[]{:S(2)}) copy-start(bf16[32,2688]{1,0:T(8,128)(2,1)S(1)} %collective-permute-done) | copy-start | bytes 516100
  62.5 33.3 %collective-permute-start.5 = (bf16[32,2688]{1,0:T(8,128)(2,1)}, bf16[32,2688]{1,0:T(8,128)(2,1)S(1)}, u32[]{:S(2)}, u32[]{:S(2)}) collective-permute-start(bf16[32,2688]{1,0:T(8,128)(2,1)} %get-tuple-element.128), channel_id=1, source_target_pairs={{0,12},{2,14},{4,8},{6,10},{8,20},{10,22},{12,16},{14,18},{16,28},... | collective-permute-start | bytes 516104 | tf_op jit(solution)/shard_map/ppermute | solution.py:489
  83.5 10.4 %copy-start.7 = (bf16[32,2688]{1,0:T(8,128)(2,1)}, bf16[32,2688]{1,0:T(8,128)(2,1)S(1)}, u32[]{:S(2)}) copy-start(bf16[32,2688]{1,0:T(8,128)(2,1)S(1)} %collective-permute-done.1) | copy-start | bytes 516100
  83.6 13.2 %collective-permute-start.6 = (bf16[32,2688]{1,0:T(8,128)(2,1)}, bf16[32,2688]{1,0:T(8,128)(2,1)S(1)}, u32[]{:S(2)}, u32[]{:S(2)}) collective-permute-start(bf16[32,2688]{1,0:T(8,128)(2,1)} %get-tuple-element.129), channel_id=1, source_target_pairs={{0,14},{2,8},{4,10},{6,12},{8,22},{10,16},{12,18},{14,20},{16,30},... | collective-permute-start | bytes 516104 | tf_op jit(solution)/shard_map/ppermute | solution.py:489
  83.6 33.8 %copy-start.8 = (bf16[32,2688]{1,0:T(8,128)(2,1)}, bf16[32,2688]{1,0:T(8,128)(2,1)S(1)}, u32[]{:S(2)}) copy-start(bf16[32,2688]{1,0:T(8,128)(2,1)S(1)} %collective-permute-done.2) | copy-start | bytes 516100
  83.6 19.1 %collective-permute-start.7 = (bf16[32,2688]{1,0:T(8,128)(2,1)}, bf16[32,2688]{1,0:T(8,128)(2,1)S(1)}, u32[]{:S(2)}, u32[]{:S(2)}) collective-permute-start(bf16[32,2688]{1,0:T(8,128)(2,1)} %get-tuple-element.130), channel_id=1, source_target_pairs={{0,16},{2,18},{4,20},{6,22},{8,24},{10,26},{12,28},{14,30},{16,0},... | collective-permute-start | bytes 516104 | tf_op jit(solution)/shard_map/ppermute | solution.py:489
  83.7 33.7 %copy-start.9 = (bf16[32,2688]{1,0:T(8,128)(2,1)}, bf16[32,2688]{1,0:T(8,128)(2,1)S(1)}, u32[]{:S(2)}) copy-start(bf16[32,2688]{1,0:T(8,128)(2,1)S(1)} %collective-permute-done.3) | copy-start | bytes 516100
  83.7 31.2 %collective-permute-start.8 = (bf16[32,2688]{1,0:T(8,128)(2,1)}, bf16[32,2688]{1,0:T(8,128)(2,1)S(1)}, u32[]{:S(2)}, u32[]{:S(2)}) collective-permute-start(bf16[32,2688]{1,0:T(8,128)(2,1)} %get-tuple-element.131), channel_id=1, source_target_pairs={{0,18},{2,20},{4,22},{6,16},{8,26},{10,28},{12,30},{14,24},{16,2},... | collective-permute-start | bytes 516104 | tf_op jit(solution)/shard_map/ppermute | solution.py:489
  89.6 27.8 %copy-start.10 = (bf16[32,2688]{1,0:T(8,128)(2,1)}, bf16[32,2688]{1,0:T(8,128)(2,1)S(1)}, u32[]{:S(2)}) copy-start(bf16[32,2688]{1,0:T(8,128)(2,1)S(1)} %collective-permute-done.4) | copy-start | bytes 516100
  89.6 25.4 %collective-permute-start.9 = (bf16[32,2688]{1,0:T(8,128)(2,1)}, bf16[32,2688]{1,0:T(8,128)(2,1)S(1)}, u32[]{:S(2)}, u32[]{:S(2)}) collective-permute-start(bf16[32,2688]{1,0:T(8,128)(2,1)} %get-tuple-element.132), channel_id=1, source_target_pairs={{0,20},{2,22},{4,16},{6,18},{8,28},{10,30},{12,24},{14,26},{16,4},... | collective-permute-start | bytes 516104 | tf_op jit(solution)/shard_map/ppermute | solution.py:489
  95.9 21.5 %copy-start.11 = (bf16[32,2688]{1,0:T(8,128)(2,1)}, bf16[32,2688]{1,0:T(8,128)(2,1)S(1)}, u32[]{:S(2)}) copy-start(bf16[32,2688]{1,0:T(8,128)(2,1)S(1)} %collective-permute-done.5) | copy-start | bytes 516100
  95.9 28.4 %collective-permute-start.10 = (bf16[32,2688]{1,0:T(8,128)(2,1)}, bf16[32,2688]{1,0:T(8,128)(2,1)}, u32[]{:S(2)}, u32[]{:S(2)}) collective-permute-start(bf16[32,2688]{1,0:T(8,128)(2,1)} %get-tuple-element.133), channel_id=1, source_target_pairs={{0,22},{2,16},{4,18},{6,20},{8,30},{10,24},{12,26},{14,28},{16,6},... | collective-permute-start | bytes 516104 | tf_op jit(solution)/shard_map/ppermute | solution.py:489
  96.8 20.6 %copy-start.12 = (bf16[32,2688]{1,0:T(8,128)(2,1)}, bf16[32,2688]{1,0:T(8,128)(2,1)S(1)}, u32[]{:S(2)}) copy-start(bf16[32,2688]{1,0:T(8,128)(2,1)S(1)} %collective-permute-done.6) | copy-start | bytes 516100
  96.8 33.1 %collective-permute-start.11 = (bf16[32,2688]{1,0:T(8,128)(2,1)}, bf16[32,2688]{1,0:T(8,128)(2,1)}, u32[]{:S(2)}, u32[]{:S(2)}) collective-permute-start(bf16[32,2688]{1,0:T(8,128)(2,1)} %get-tuple-element.134), channel_id=1, source_target_pairs={{0,24},{2,26},{4,28},{6,30},{8,0},{10,2},{12,4},{14,6},{16,8},{18,... | collective-permute-start | bytes 516104 | tf_op jit(solution)/shard_map/ppermute | solution.py:489
  102.7 14.7 %copy-start.13 = (bf16[32,2688]{1,0:T(8,128)(2,1)}, bf16[32,2688]{1,0:T(8,128)(2,1)S(1)}, u32[]{:S(2)}) copy-start(bf16[32,2688]{1,0:T(8,128)(2,1)S(1)} %collective-permute-done.7) | copy-start | bytes 516100
  102.7 27.2 %collective-permute-start.12 = (bf16[32,2688]{1,0:T(8,128)(2,1)}, bf16[32,2688]{1,0:T(8,128)(2,1)}, u32[]{:S(2)}, u32[]{:S(2)}) collective-permute-start(bf16[32,2688]{1,0:T(8,128)(2,1)} %get-tuple-element.135), channel_id=1, source_target_pairs={{0,26},{2,28},{4,30},{6,24},{8,2},{10,4},{12,6},{14,0},{16,10},{18... | collective-permute-start | bytes 516104 | tf_op jit(solution)/shard_map/ppermute | solution.py:489
  114.9 2.5 %copy-start.14 = (bf16[32,2688]{1,0:T(8,128)(2,1)}, bf16[32,2688]{1,0:T(8,128)(2,1)S(1)}, u32[]{:S(2)}) copy-start(bf16[32,2688]{1,0:T(8,128)(2,1)S(1)} %collective-permute-done.8) | copy-start | bytes 516100
  114.9 15.0 %collective-permute-start.13 = (bf16[32,2688]{1,0:T(8,128)(2,1)}, bf16[32,2688]{1,0:T(8,128)(2,1)}, u32[]{:S(2)}, u32[]{:S(2)}) collective-permute-start(bf16[32,2688]{1,0:T(8,128)(2,1)} %get-tuple-element.136), channel_id=1, source_target_pairs={{0,28},{2,30},{4,24},{6,26},{8,4},{10,6},{12,0},{14,2},{16,12},{18... | collective-permute-start | bytes 516104 | tf_op jit(solution)/shard_map/ppermute | solution.py:489
  115.0 2.4 %copy-start.15 = (bf16[32,2688]{1,0:T(8,128)(2,1)}, bf16[32,2688]{1,0:T(8,128)(2,1)S(1)}, u32[]{:S(2)}) copy-start(bf16[32,2688]{1,0:T(8,128)(2,1)S(1)} %collective-permute-done.9) | copy-start | bytes 516100
  115.0 18.1 %collective-permute-start.14 = (bf16[32,2688]{1,0:T(8,128)(2,1)}, bf16[32,2688]{1,0:T(8,128)(2,1)}, u32[]{:S(2)}, u32[]{:S(2)}) collective-permute-start(bf16[32,2688]{1,0:T(8,128)(2,1)} %get-tuple-element.137), channel_id=1, source_target_pairs={{0,30},{2,24},{4,26},{6,28},{8,6},{10,0},{12,2},{14,4},{16,14},{18... | collective-permute-start | bytes 516104 | tf_op jit(solution)/shard_map/ppermute | solution.py:489
  124.2 11.1 %collective-permute-start.15 = (f32[4,2560]{1,0:T(4,128)}, f32[4,2560]{1,0:T(4,128)S(1)}, u32[]{:S(2)}, u32[]{:S(2)}) collective-permute-start(f32[4,2560]{1,0:T(4,128)} %select_maximum_fusion), channel_id=1, source_target_pairs={{2,0},{4,2},{6,4},{8,6},{10,8},{12,10},{14,12},{16,14},{18,16},{20... | collective-permute-start | bytes 122888 | tf_op jit(solution)/shard_map/ppermute | solution.py:461
